TPU v7x, 32 devices: a whole 2x2x4 slice. The times are simulated.
32 devices in a mesh: fsdp: 4 (over z), ctx: 2 (over x), tp: 4 (over y, core).
Axes of the slice: x: 2, y: 2, z: 4, core: 2. Of those that a mesh axis runs over, the one named last changes fastest.
Arguments:
- residual: bfloat16 [8, 1024, 1024], P('fsdp', ('ctx', 'tp')), may hold values from -6 to 6
- query_weight: bfloat16 [1024, 1024], P('fsdp', 'tp'), may hold values from -0.1875 to 0.1875
- key_weight: bfloat16 [1024, 1024], P('fsdp', 'tp'), may hold values from -0.1875 to 0.1875
- value_weight: bfloat16 [1024, 1024], P('fsdp', 'tp'), may hold values from -0.1875 to 0.1875
- output_weight: bfloat16 [1024, 1024], P('tp', 'fsdp'), may hold values from -0.1875 to 0.1875
- sharpness: float32 [1024], P('tp'), may hold values from 1 to 1.8
- attend_rate: float32 [1024], replicated, may hold values from 0.15 to 0.9
- up_weight: bfloat16 [1024, 4096], P('fsdp', 'tp'), may hold values from -0.1875 to 0.1875
- gate_weight: bfloat16 [1024, 4096], P('fsdp', 'tp'), may hold values from -0.1875 to 0.1875
- down_weight: bfloat16 [4096, 1024], P('tp', 'fsdp'), may hold values from -0.09375 to 0.09375
- amplitude: float32 [4096], P('tp'), may hold values from 0.5 to 2
- steepness: float32 [4096], P('tp'), may hold values from 0.5 to 2
- mixer_rate: float32 [1024], replicated, may hold values from 0.15 to 0.9
- block_ids: int32 [8, 1024], P('fsdp'), may hold values from 0 to 4, as said below
- positions: int32 [8, 1024], P('fsdp', 'ctx'), may hold values from 0 to 4095
- cotangent: bfloat16 [8, 1024, 1024], P('fsdp', ('ctx', 'tp')), may hold values from -6 to 6
Outputs:
- layer_out: bfloat16 [8, 1024, 1024], P('fsdp', ('ctx', 'tp'))
- grad_input: float32 [8, 1024, 1024], P('fsdp', ('ctx', 'tp'))
- grad_query: float32 [1024, 1024], P('fsdp', 'tp')
- grad_key: float32 [1024, 1024], P('fsdp', 'tp')
- grad_value: float32 [1024, 1024], P('fsdp', 'tp')
- grad_output: float32 [1024, 1024], P('tp', 'fsdp')
- grad_sharpness: float32 [1024], replicated
- grad_attend: float32 [1024], replicated
- grad_up: float32 [1024, 4096], P('fsdp', 'tp')
- grad_gate: float32 [1024, 4096], P('fsdp', 'tp')
- grad_down: float32 [4096, 1024], P('tp', 'fsdp')
- grad_amplitude: float32 [4096], replicated
- grad_steepness: float32 [4096], replicated
- grad_mixer: float32 [1024], replicated
Inputs may be any that keep to these rules, and one draw needn't show every extreme that they name: `block_ids`: in each sequence the block id of the token at index t is (t + offset) // 256, with an offset of 1 to 255 drawn for each sequence: full blocks of 256 tokens, a shorter first and last block.
All inputs are finite; a program needn't handle non-finite values.
Results may differ from a plain program's by a relative error of at most 0.02.
Values may be sent and summed in bfloat16 or wider, within the bound.
A program may use at most 128 MiB of HBM per device.

v0:
```python
import functools
import math

import jax
import jax.numpy as jnp
from jax import lax
from jax.experimental import pallas as pl
from jax.experimental.pallas import tpu as pltpu
from jax.sharding import PartitionSpec as P

HD = 64
norm_eps = 1e-06
rope_base = 10000.0
BF = jnp.bfloat16
F32 = jnp.float32
MESH = pl.DeviceIdType.MESH
IN_VMEM = pl.BlockSpec(memory_space=pltpu.VMEM)


def remote(source, target, send, receive, **where):
    return pltpu.make_async_remote_copy(
        src_ref=source,
        dst_ref=target,
        send_sem=send,
        recv_sem=receive,
        device_id=where,
        device_id_type=MESH,
    )


def meet(peers):
    barrier = pltpu.get_barrier_semaphore()
    for where in peers:
        pl.semaphore_signal(barrier, inc=1, device_id=where, device_id_type=MESH)
    pl.semaphore_wait(barrier, len(peers))


def tensor_peers():
    me = lax.axis_index("tp")
    core = lax.rem(me, 2)
    chip = lax.div(me, 2)
    return (
        me,
        chip * 2 + (1 - core),
        (1 - chip) * 2 + core,
        (1 - chip) * 2 + (1 - core),
    )


def row_chunks(halves, rows, parts):
    step = rows // parts
    return [(h, pl.ds(i * step, step)) for h in range(halves) for i in range(parts)]


def gather_kernel(chunks, x_ref, out_ref, local_sem, send, receive):
    me, partner, across, _ = tensor_peers()
    meet([{"tp": partner}, {"tp": across}])
    own = pltpu.make_async_copy(x_ref, out_ref.at[:, me], local_sem)
    own.start()
    count = len(chunks)
    over, side, relay = [], [], []
    for i, (h, rows) in enumerate(chunks):
        over.append(
            remote(
                x_ref.at[h, rows],
                out_ref.at[h, me, rows],
                send.at[i],
                receive.at[i],
                tp=across,
            )
        )
        over[-1].start()
    for i, (h, rows) in enumerate(chunks):
        side.append(
            remote(
                x_ref.at[h, rows],
                out_ref.at[h, me, rows],
                send.at[count + i],
                receive.at[count + i],
                tp=partner,
            )
        )
        side[-1].start()
    for i, (h, rows) in enumerate(chunks):
        over[i].wait_recv()
        relay.append(
            remote(
                out_ref.at[h, across, rows],
                out_ref.at[h, across, rows],
                send.at[2 * count + i],
                receive.at[2 * count + i],
                tp=partner,
            )
        )
        relay[-1].start()
    for i in range(count):
        side[i].wait_recv()
        relay[i].wait_recv()
    for i in range(count):
        over[i].wait_send()
        side[i].wait_send()
        relay[i].wait_send()
    own.wait()


def tensor_gather(values):
    halves, rows, width = values.shape
    chunks = row_chunks(halves, rows, 2)
    return pl.pallas_call(
        functools.partial(gather_kernel, chunks),
        out_shape=jax.ShapeDtypeStruct((halves, 4, rows, width), values.dtype),
        in_specs=[IN_VMEM],
        out_specs=IN_VMEM,
        scratch_shapes=[
            pltpu.SemaphoreType.DMA,
            pltpu.SemaphoreType.DMA((3 * len(chunks),)),
            pltpu.SemaphoreType.DMA((3 * len(chunks),)),
        ],
        compiler_params=pltpu.CompilerParams(collective_id=0, has_side_effects=True),
        cost_estimate=pl.CostEstimate(flops=0, bytes_accessed=40_000_000, transcendentals=0),
        name="tensor_gather",
    )(values)


def scatter_kernel(chunks, p_ref, out_ref, pair, mine, far, joined, send, receive):
    me, partner, across, diagonal = tensor_peers()
    meet([{"tp": partner}, {"tp": across}])
    count = len(chunks)
    first, second, third = [], [], []
    for i, (h, rows) in enumerate(chunks):
        first.append(
            remote(
                p_ref.at[h, diagonal, rows],
                pair.at[h, rows],
                send.at[i],
                receive.at[i],
                tp=partner,
            )
        )
        first[-1].start()
    for i, (h, rows) in enumerate(chunks):
        second.append(
            remote(
                p_ref.at[h, partner, rows],
                mine.at[h, rows],
                send.at[count + i],
                receive.at[count + i],
                tp=partner,
            )
        )
        second[-1].start()
    for i, (h, rows) in enumerate(chunks):
        first[i].wait_recv()
        joined[h, rows] = (
            p_ref[h, across, rows].astype(F32) + pair[h, rows].astype(F32)
        ).astype(BF)
        third.append(
            remote(
                joined.at[h, rows],
                far.at[h, rows],
                send.at[2 * count + i],
                receive.at[2 * count + i],
                tp=across,
            )
        )
        if i > 0:
            third[i - 1].start()
    for i, (h, rows) in enumerate(chunks):
        second[i].wait_recv()
        out_ref[h, rows] = p_ref[h, me, rows].astype(F32) + mine[h, rows].astype(F32)
        if i == 0:
            third[-1].start()
    for i, (h, rows) in enumerate(chunks):
        third[i].wait_recv()
        out_ref[h, rows] += far[h, rows].astype(F32)
    for i in range(count):
        first[i].wait_send()
        second[i].wait_send()
        third[i].wait_send()


def tensor_scatter(partial):
    halves, _, rows, width = partial.shape
    chunks = row_chunks(halves, rows, 2)
    block = pltpu.VMEM((halves, rows, width), BF)
    return pl.pallas_call(
        functools.partial(scatter_kernel, chunks),
        out_shape=jax.ShapeDtypeStruct((halves, rows, width), F32),
        in_specs=[IN_VMEM],
        out_specs=IN_VMEM,
        scratch_shapes=[block] * 4
        + [
            pltpu.SemaphoreType.DMA((3 * len(chunks),)),
            pltpu.SemaphoreType.DMA((3 * len(chunks),)),
        ],
        compiler_params=pltpu.CompilerParams(collective_id=1, has_side_effects=True),
        cost_estimate=pl.CostEstimate(flops=0, bytes_accessed=40_000_000, transcendentals=0),
        name="tensor_scatter",
    )(partial)


def opening_kernel(
    n, x_ref, q_ref, k_ref, v_ref, o_ref, out_ref, qkv_ref, full_o_ref, local, send, receive
):
    me, partner, across, _ = tensor_peers()
    ctx = lax.axis_index("ctx")
    other = 1 - ctx
    z = lax.axis_index("fsdp")
    weights = [(q_ref, 0), (k_ref, 1), (v_ref, 2)]
    rows_w = q_ref.shape[0]
    cols_w = q_ref.shape[1]
    half = rows_w // 2
    o_half = o_ref.shape[0] // 2
    o_cols = o_ref.shape[1]
    others = [lax.rem(z + d, n) for d in range(1, n)]
    meet(
        [{"tp": partner}, {"tp": across}, {"ctx": other}] + [{"fsdp": target} for target in others]
    )
    used = [0]

    def launch(source, target, **where):
        i = used[0]
        used[0] += 1
        copy = remote(source, target, send.at[i], receive.at[i], **where)
        copy.start()
        return copy

    def weight_rows(h):
        return pl.ds(pl.multiple_of(h * half, half), half)

    def output_rows(h):
        return pl.ds(pl.multiple_of(h * o_half, o_half), o_half)

    def output_cols(block):
        return pl.ds(pl.multiple_of(block * o_cols, o_cols), o_cols)

    swap = launch(x_ref.at[other], out_ref.at[ctx, me], ctx=other)
    over = [launch(x_ref.at[ctx], out_ref.at[ctx, me], tp=across)]
    side = [launch(x_ref.at[ctx], out_ref.at[ctx, me], tp=partner)]
    along = {}
    order = sorted(range(1, n), key=lambda d: min(d, n - d))
    for d in order:
        target = others[d - 1]
        group = []
        for ref, at in weights:
            group.append(
                launch(
                    ref.at[weight_rows(ctx)],
                    qkv_ref.at[z, weight_rows(ctx), pl.ds(at * cols_w, cols_w)],
                    fsdp=target,
                )
            )
        group.append(
            launch(
                o_ref.at[output_rows(ctx)],
                full_o_ref.at[output_rows(ctx), output_cols(z)],
                fsdp=target,
            )
        )
        along[d] = group
    own = [pltpu.make_async_copy(x_ref.at[ctx], out_ref.at[ctx, me], local.at[0])]
    for ref, at in weights:
        own.append(
            pltpu.make_async_copy(
                ref, qkv_ref.at[z, :, pl.ds(at * cols_w, cols_w)], local.at[1 + at]
            )
        )
    own.append(pltpu.make_async_copy(o_ref, full_o_ref.at[:, output_cols(z)], local.at[4]))
    for copy in own:
        copy.start()
    swap.wait_recv()
    over.append(launch(out_ref.at[other, me], out_ref.at[other, me], tp=across))
    side.append(launch(out_ref.at[other, me], out_ref.at[other, me], tp=partner))
    over[0].wait_recv()
    relay = [launch(out_ref.at[ctx, across], out_ref.at[ctx, across], tp=partner)]
    handed = []
    for d in order:
        for copy in along[d]:
            copy.wait_recv()
        block = lax.rem(z + n - d, n)
        handed.append(
            launch(
                qkv_ref.at[block, weight_rows(ctx)],
                qkv_ref.at[block, weight_rows(ctx)],
                ctx=other,
            )
        )
        handed.append(
            launch(
                full_o_ref.at[output_rows(ctx), output_cols(block)],
                full_o_ref.at[output_rows(ctx), output_cols(block)],
                ctx=other,
            )
        )
        if d == order[0]:
            over[1].wait_recv()
            relay.append(launch(out_ref.at[other, across], out_ref.at[other, across], tp=partner))
    for copy in side + relay + handed:
        copy.wait_recv()
    for copy in [swap] + over + side + relay + handed:
        copy.wait_send()
    for d in order:
        for copy in along[d]:
            copy.wait_send()
    for copy in own:
        copy.wait()


def opening(n, rows, query, key, value, output):
    _, count, width = rows.shape
    copies = 7 + 6 * (n - 1)
    gathered, qkv, full_output = pl.pallas_call(
        functools.partial(opening_kernel, n),
        out_shape=(
            jax.ShapeDtypeStruct((2, 4, count, width), BF),
            jax.ShapeDtypeStruct((n, query.shape[0], 3 * query.shape[1]), BF),
            jax.ShapeDtypeStruct((output.shape[0], n * output.shape[1]), BF),
        ),
        in_specs=[IN_VMEM] * 5,
        out_specs=(IN_VMEM,) * 3,
        scratch_shapes=[
            pltpu.SemaphoreType.DMA((5,)),
            pltpu.SemaphoreType.DMA((copies,)),
            pltpu.SemaphoreType.DMA((copies,)),
        ],
        compiler_params=pltpu.CompilerParams(collective_id=2, has_side_effects=True),
        cost_estimate=pl.CostEstimate(flops=0, bytes_accessed=60_000_000, transcendentals=0),
        name="opening",
    )(rows, query, key, value, output)
    return gathered, qkv.reshape(n * query.shape[0], 3 * query.shape[1]), full_output


def grads_kernel(
    n,
    g_ref,
    v_ref,
    down_ref,
    ug_ref,
    input_ref,
    out_ref,
    sums_ref,
    full_down_ref,
    full_ug_ref,
    traded_ref,
    arrived,
    reduced,
    far,
    total,
    pair,
    joined,
    group,
    send,
    receive,
    vector_send,
    vector_receive,
    share_send,
    share_receive,
    local,
):
    me, _, _, _ = tensor_peers()
    ctx = lax.axis_index("ctx")
    other = 1 - ctx
    z = lax.axis_index("fsdp")
    blocks = [lax.rem(z + d, n) for d in range(n)]
    around = [lax.rem(me + d, 4) for d in range(1, 4)]
    meet(
        [{"ctx": other}]
        + [{"fsdp": block} for block in blocks[1:]]
        + [{"tp": index} for index in around]
    )
    swap = remote(v_ref, pair, vector_send.at[0], vector_receive.at[0], ctx=other)
    swap.start()
    order = sorted(range(1, n), key=lambda d: -min(d, n - d)) + [0]
    near = {}
    for d in order:
        near[d] = remote(
            g_ref.at[blocks[d], other], arrived.at[d], send.at[d], receive.at[d], ctx=other
        )
        near[d].start()
    shares = [
        remote(input_ref.at[other], traded_ref.at[ctx], share_send.at[0], share_receive.at[0], ctx=other),
        remote(down_ref, full_down_ref.at[ctx], share_send.at[1], share_receive.at[1], ctx=other),
        remote(ug_ref, full_ug_ref.at[ctx], share_send.at[2], share_receive.at[2], ctx=other),
    ]
    own = [
        pltpu.make_async_copy(input_ref.at[ctx], traded_ref.at[ctx], local.at[0]),
        pltpu.make_async_copy(down_ref, full_down_ref.at[ctx], local.at[1]),
        pltpu.make_async_copy(ug_ref, full_ug_ref.at[ctx], local.at[2]),
    ]
    for copy in shares + own:
        copy.start()
    swap.wait_recv()
    joined[...] = v_ref[...] + pair[...]
    group[z] = joined[...]
    line = [
        remote(joined, group.at[z], vector_send.at[d], vector_receive.at[d], fsdp=blocks[d])
        for d in range(1, n)
    ]
    along = {}
    for step, d in enumerate(order):
        near[d].wait_recv()
        value = g_ref[blocks[d], ctx].astype(F32) + arrived[d].astype(F32)
        if d:
            reduced[d] = value.astype(BF)
            along[d] = remote(
                reduced.at[d], far.at[d], send.at[n + d], receive.at[n + d], fsdp=blocks[d]
            )
        else:
            total[...] = value
        if step:
            along[order[step - 1]].start()
        if step == 0:
            for copy in line:
                copy.start()
    for copy in line:
        copy.wait_recv()
    summed = group[0]
    for i in range(1, n):
        summed = summed + group[i]
    sums_ref[me] = summed
    ring = [
        remote(
            sums_ref.at[me],
            sums_ref.at[me],
            vector_send.at[n + i],
            vector_receive.at[n + i],
            tp=index,
        )
        for i, index in enumerate(around)
    ]
    for step, d in enumerate(order[:-1]):
        along[d].wait_recv()
        total[...] += far[d].astype(F32)
        if step == 0:
            for copy in ring:
                copy.start()
    out_ref[ctx] = total[...].astype(BF)
    last = remote(out_ref.at[ctx], out_ref.at[ctx], send.at[n], receive.at[n], ctx=other)
    for d in order:
        near[d].wait_send()
    last.start()
    for d in order[:-1]:
        along[d].wait_send()
    for copy in ring + shares:
        copy.wait_recv()
    for copy in [swap] + line + ring + shares:
        copy.wait_send()
    for copy in own:
        copy.wait()
    last.wait_recv()
    last.wait_send()


def sum_grads(n, parts, vectors, down_share, ug_share, traded):
    total_rows, width = parts.shape
    rows = total_rows // (2 * n)
    vector = pltpu.VMEM(vectors.shape, F32)
    out, sums, down, ug, traded = pl.pallas_call(
        functools.partial(grads_kernel, n),
        out_shape=(
            jax.ShapeDtypeStruct((2, rows, width), BF),
            jax.ShapeDtypeStruct((4,) + vectors.shape, F32),
            jax.ShapeDtypeStruct((2,) + down_share.shape, BF),
            jax.ShapeDtypeStruct((2,) + ug_share.shape, BF),
            jax.ShapeDtypeStruct(traded.shape, BF),
        ),
        in_specs=[IN_VMEM] * 5,
        out_specs=(IN_VMEM,) * 5,
        scratch_shapes=[
            pltpu.VMEM((n, rows, width), BF),
            pltpu.VMEM((n, rows, width), BF),
            pltpu.VMEM((n, rows, width), BF),
            pltpu.VMEM((rows, width), F32),
            vector,
            vector,
            pltpu.VMEM((n,) + vectors.shape, F32),
            pltpu.SemaphoreType.DMA((2 * n,)),
            pltpu.SemaphoreType.DMA((2 * n,)),
            pltpu.SemaphoreType.DMA((n + 3,)),
            pltpu.SemaphoreType.DMA((n + 3,)),
            pltpu.SemaphoreType.DMA((3,)),
            pltpu.SemaphoreType.DMA((3,)),
            pltpu.SemaphoreType.DMA((3,)),
        ],
        compiler_params=pltpu.CompilerParams(collective_id=3, has_side_effects=True),
        cost_estimate=pl.CostEstimate(flops=0, bytes_accessed=120_000_000, transcendentals=0),
        name="sum_grads",
    )(parts.reshape(n, 2, rows, width), vectors, down_share, ug_share, traded)
    return (
        out.reshape(2 * rows, width),
        sums,
        down.reshape(-1, down.shape[2]),
        ug.reshape(-1, ug.shape[2]),
        traded,
    )


def unit_rows(values):
    return values * lax.rsqrt(jnp.mean(values * values, axis=-1, keepdims=True) + norm_eps)


def rotate_pairs(values, angles):
    middle = values.shape[-1] // 2
    leading = values[..., :middle]
    trailing = values[..., middle:]
    cosine = jnp.cos(angles)[..., None, :]
    sine_part = jnp.sin(angles)[..., None, :]
    return jnp.concatenate(
        [leading * cosine - trailing * sine_part, trailing * cosine + leading * sine_part], axis=-1
    )


def angles_for(positions, head_size):
    middle = head_size // 2
    frequency = rope_base ** (-2.0 * jnp.arange(middle).astype(F32) / head_size)
    return positions.astype(F32)[..., None] * frequency


def prepare_heads(projected, angles, gains, head_size):
    heads_here = projected.shape[-1] // head_size
    shaped = projected.reshape(projected.shape[:-1] + (heads_here, head_size))
    normed = unit_rows(rotate_pairs(shaped, angles)) * gains.reshape(heads_here, head_size)
    return normed.reshape(projected.shape)


def product(left, right):
    return jnp.dot(left, right, preferred_element_type=F32)


def transposed_left(left, right):
    return lax.dot_general(left, right, (((0,), (0,)), ((), ())), preferred_element_type=F32)


def transposed_right(left, right):
    return lax.dot_general(left, right, (((1,), (1,)), ((), ())), preferred_element_type=F32)


def branch_mix(branch, base, rate):
    return unit_rows(base + rate * (unit_rows(branch) - base))


def activate(upper, gated_raw, amplitude, steepness):
    scaled = gated_raw * steepness
    return upper * amplitude * (scaled * jax.nn.sigmoid(scaled))


def trade(values, sizes):
    n = sizes["ctx"]
    me = lax.axis_index("ctx")
    if n == 2:
        own = lax.dynamic_index_in_dim(values, me, 0, keepdims=False)
        other = lax.dynamic_index_in_dim(values, 1 - me, 0, keepdims=False)
        got = lax.ppermute(other, "ctx", [(0, 1), (1, 0)])
        first = jnp.where(me == 0, own, got)
        second = jnp.where(me == 0, got, own)
        return jnp.stack([first, second])
    return lax.all_to_all(values, "ctx", split_axis=0, concat_axis=0, tiled=True)


def swap_halves(share, ctx):
    got = lax.ppermute(share, "ctx", [(0, 1), (1, 0)])
    first = jnp.where(ctx == 0, share, got)
    second = jnp.where(ctx == 0, got, share)
    return jnp.concatenate([first, second], axis=0)


def attend_both(query_low, key_low, value_low, ids):
    length, width = query_low.shape
    heads = width // HD
    q = query_low.reshape(length, heads, HD)
    k = key_low.reshape(length, heads, HD)
    v = value_low.reshape(length, heads, HD)
    scores = jnp.einsum("qhd,khd->hqk", q, k, preferred_element_type=F32) / math.sqrt(HD)
    allowed = ids[None, :] <= ids[:, None]
    scores = jnp.where(allowed[None], scores, -1e30)
    row_max = jnp.max(scores, axis=-1, keepdims=True)
    exponent = jnp.exp(scores - row_max)
    row_total = jnp.sum(exponent, axis=-1, keepdims=True)
    weights_low = (exponent / row_total).astype(BF)
    out = jnp.einsum("hqk,khd->qhd", weights_low, v, preferred_element_type=F32)
    return out.reshape(length, width).astype(BF), (row_max + jnp.log(row_total))[..., 0]


def attend_back(query_low, key_low, value_low, ids, logsum, grad):
    length, width = query_low.shape
    heads = width // HD
    q = query_low.reshape(length, heads, HD)
    k = key_low.reshape(length, heads, HD)
    v = value_low.reshape(length, heads, HD)
    g = grad.reshape(length, heads, HD)
    scores = jnp.einsum("qhd,khd->hqk", q, k, preferred_element_type=F32) / math.sqrt(HD)
    allowed = ids[None, :] <= ids[:, None]
    scores = jnp.where(allowed[None], scores, -1e30)
    soft = jnp.exp(scores - logsum[..., None])
    grad_v = jnp.einsum("hqk,qhd->khd", soft.astype(BF), g, preferred_element_type=F32)
    grad_w = jnp.einsum("qhd,khd->hqk", g, v, preferred_element_type=F32)
    grad_s = soft * (grad_w - jnp.sum(grad_w * soft, axis=-1, keepdims=True))
    low = grad_s.astype(BF)
    grad_q = jnp.einsum("hqk,khd->qhd", low, k, preferred_element_type=F32) / math.sqrt(HD)
    grad_k = jnp.einsum("hqk,qhd->khd", low, q, preferred_element_type=F32) / math.sqrt(HD)
    return (
        grad_q.reshape(length, width),
        grad_k.reshape(length, width),
        grad_v.reshape(length, width),
    )


def per_device(sizes):
    def run(
        residual,
        query_weight,
        key_weight,
        value_weight,
        output_weight,
        sharpness,
        attend_rate,
        up_weight,
        gate_weight,
        down_weight,
        amplitude,
        steepness,
        mixer_rate,
        block_ids,
        positions,
        cotangent,
    ):
        n = sizes["fsdp"]
        tp = sizes["tp"]
        rows, width = residual.shape[1:]
        hidden_here = up_weight.shape[1]
        heads_width = query_weight.shape[1]
        small = n <= 4
        shape4 = (2, tp, rows, width)

        ctx = lax.axis_index("ctx")

        def own_half(shard):
            half = shard.shape[0] // 2
            return lax.dynamic_slice_in_dim(shard, ctx * half, half, 0)

        ug_half = own_half(jnp.concatenate([up_weight, gate_weight], axis=1))
        down_half = own_half(down_weight.T)
        if small:
            gathered, full_qkv, full_output = opening(
                n, residual, query_weight, key_weight, value_weight, output_weight
            )
            gathered, ug_half, down_half = lax.optimization_barrier((gathered, ug_half, down_half))
            tensor_index = lax.axis_index("tp")
            mine = lax.dynamic_index_in_dim(gathered, tensor_index, 1, keepdims=False)
        else:
            mine = trade(residual, sizes)
            qkv_shard = jnp.concatenate([query_weight, key_weight, value_weight], axis=1)
            full_qkv = lax.all_gather(qkv_shard, "fsdp", axis=0, tiled=True)
            full_output = lax.all_gather(output_weight, "fsdp", axis=1, tiled=True)
            gathered = tensor_gather(mine)
        full_ug = lax.all_gather(ug_half, ("fsdp", "ctx"), axis=0, tiled=True)
        full_down = lax.all_gather(down_half, ("fsdp", "ctx"), axis=0, tiled=True)

        ids = lax.dynamic_index_in_dim(block_ids, ctx, 0, keepdims=False)
        my_positions = trade(positions, sizes).reshape(-1)
        angles = angles_for(my_positions, HD)

        flat_in = gathered.reshape(-1, width)
        raw = product(flat_in, full_qkv)
        raw_query, raw_key, raw_value = jnp.split(raw, 3, axis=1)

        def prepare_local(projected, gains):
            return prepare_heads(projected, angles, gains, HD)

        query_ready, query_back = jax.vjp(prepare_local, raw_query, sharpness)
        key_ready, key_back = jax.vjp(prepare_local, raw_key, sharpness)
        query_low = query_ready.astype(BF)
        key_low = key_ready.astype(BF)
        value_low = raw_value.astype(BF)
        attended, logsum = attend_both(query_low, key_low, value_low, ids)

        def reduce_rows(partial):
            return tensor_scatter(partial.astype(BF).reshape(shape4))

        def gather_rows(values):
            return tensor_gather(values.astype(BF)).reshape(-1, width)

        attend_sum = reduce_rows(product(attended, full_output))
        residual_float = mine.astype(F32)
        first, attend_back_mix = jax.vjp(branch_mix, attend_sum, residual_float, attend_rate)
        first_all = gather_rows(first)
        ug_raw = product(first_all, full_ug)
        up_raw, gate_raw = ug_raw[:, :hidden_here], ug_raw[:, hidden_here:]
        hidden, activate_back = jax.vjp(activate, up_raw, gate_raw, amplitude, steepness)
        hidden_low = hidden.astype(BF)
        down_sum = reduce_rows(transposed_right(hidden_low, full_down))
        outcome, mixer_back = jax.vjp(branch_mix, down_sum, first, mixer_rate)
        layer_out = trade(outcome.astype(BF), sizes)
        my_cot = trade(cotangent, sizes)
        grad_down_sum, grad_first, grad_mixer_part = mixer_back(my_cot.astype(F32))
        down_grad_all = gather_rows(grad_down_sum)
        grad_hidden = product(down_grad_all, full_down)
        grad_down_part = transposed_left(down_grad_all, hidden_low)
        grad_up_raw, grad_gate_raw, grad_amplitude_part, grad_steepness_part = activate_back(
            grad_hidden
        )
        ug_grad = jnp.concatenate([grad_up_raw.astype(BF), grad_gate_raw.astype(BF)], axis=1)
        grad_first = grad_first + reduce_rows(transposed_right(ug_grad, full_ug))
        grad_ug_part = transposed_left(first_all, ug_grad)
        grad_attend_sum, grad_residual, grad_attend_part = attend_back_mix(grad_first)
        attend_grad_all = gather_rows(grad_attend_sum)
        grad_output_part = transposed_left(attend_grad_all, attended)
        grad_attended = transposed_right(attend_grad_all, full_output).astype(BF)
        grad_query_ready, grad_key_ready, grad_value_ready = attend_back(
            query_low, key_low, value_low, ids, logsum, grad_attended
        )
        grad_raw_query, sharp_query = query_back(grad_query_ready)
        grad_raw_key, sharp_key = key_back(grad_key_ready)
        qkv_grad = jnp.concatenate(
            [grad_raw_query.astype(BF), grad_raw_key.astype(BF), grad_value_ready.astype(BF)], axis=1
        )
        grad_input = grad_residual + reduce_rows(transposed_right(qkv_grad, full_qkv))
        grad_input = grad_input.astype(BF)
        grad_qkv_part = transposed_left(flat_in, qkv_grad)

        def scatter_rows(part):
            return lax.psum_scatter(
                part.astype(BF), ("fsdp", "ctx"), scatter_dimension=0, tiled=True
            )

        vectors = [
            sharp_query + sharp_key,
            grad_amplitude_part,
            grad_steepness_part,
            grad_attend_part,
            grad_mixer_part,
        ]
        lengths = [vector.shape[0] for vector in vectors]
        packed = jnp.concatenate(vectors)
        packed = jnp.pad(packed, (0, -packed.shape[0] % 1024)).reshape(-1, 128)
        down_share = scatter_rows(grad_down_part)
        ug_share = scatter_rows(grad_ug_part)
        late = jnp.concatenate([grad_qkv_part.astype(BF), grad_output_part.astype(BF)], axis=1)
        if small:
            late, sums, grad_down, grad_ug, grad_input = sum_grads(
                n, late, packed, down_share, ug_share, grad_input
            )
        else:
            late = swap_halves(scatter_rows(late), ctx)
            sums = lax.all_gather(lax.psum(packed, ("fsdp", "ctx")), "tp", axis=0)
            grad_down = swap_halves(down_share, ctx)
            grad_ug = swap_halves(ug_share, ctx)
            grad_input = trade(grad_input, sizes)
        late = late.astype(F32)
        grad_down = grad_down.astype(F32).T
        grad_ug = grad_ug.astype(F32)
        grad_input = grad_input.astype(F32)
        grad_up, grad_gate = grad_ug[:, :hidden_here], grad_ug[:, hidden_here:]
        grad_query, grad_key, grad_value = jnp.split(late[:, : 3 * heads_width], 3, axis=1)
        grad_output = late[:, 3 * heads_width :].T
        sums = sums.reshape(tp, -1)
        pieces = []
        start = 0
        for length in lengths:
            pieces.append(sums[:, start : start + length])
            start += length
        grad_sharpness, grad_amplitude, grad_steepness = [p.reshape(-1) for p in pieces[:3]]
        grad_attend, grad_mixer = [p.sum(axis=0) for p in pieces[3:]]
        return (
            layer_out,
            grad_input,
            grad_query,
            grad_key,
            grad_value,
            grad_output,
            grad_sharpness,
            grad_attend,
            grad_up,
            grad_gate,
            grad_down,
            grad_amplitude,
            grad_steepness,
            grad_mixer,
        )

    return run


def solution(mesh):
    return jax.shard_map(
        per_device(dict(mesh.shape)),
        mesh=mesh,
        in_specs=(
            P("fsdp", ("ctx", "tp"), None),
            P("fsdp", "tp"),
            P("fsdp", "tp"),
            P("fsdp", "tp"),
            P("tp", "fsdp"),
            P("tp"),
            P(),
            P("fsdp", "tp"),
            P("fsdp", "tp"),
            P("tp", "fsdp"),
            P("tp"),
            P("tp"),
            P(),
            P("fsdp", None),
            P("fsdp", "ctx"),
            P("fsdp", ("ctx", "tp"), None),
        ),
        out_specs=(
            P("fsdp", ("ctx", "tp"), None),
            P("fsdp", ("ctx", "tp"), None),
            P("fsdp", "tp"),
            P("fsdp", "tp"),
            P("fsdp", "tp"),
            P("tp", "fsdp"),
            P(),
            P(),
            P("fsdp", "tp"),
            P("fsdp", "tp"),
            P("tp", "fsdp"),
            P(),
            P(),
            P(),
        ),
        check_vma=False,
    )
```

profile of v0, /device:TPU:0, one launch (start us, length us, event | category | flops | bytes accessed | tf_op | source)
XLA Modules:
  0.0 469.2 jit_solution(9242906502925091146)
XLA Ops:
  7.3 1.0 copy-done
  8.9 1.9 fusion.22
  10.8 39.3 %opening.1 = (bf16[2,4,128,1024]{3,2,1,0:T(8,128)(2,1)}, bf16[4,256,768]{2,1,0:T(8,128)(2,1)}, bf16[256,1024]{1,0:T(8,128)(2,1)}) custom-call(bf16[2,128,1024]{2,1,0:T(8,128)(2,1)} %x_ref.1, bf16[256,256]{1,0:T(8,128)(2,1)} %q_ref.1, bf16[256,256]{1,0:T(8,128)(2,1)} %k_ref.1, bf16[256,256]{1,0:T(8,128)(2,1)} %v_ref.1, bf16[256,256]{1,0:T(8,128)(2,1)} %o_ref.1), custom_call_target="tpu_custom_call" | custom-call | bytes 60000000 | tf_op jit(solution)/shard_map/opening/pallas_call | solution.py:312
  51.6 1.7 dynamic-slice_bitcast_fusion
  53.2 1.5 collective-permute-start.2
  55.5 1.6 broadcast_compare_fusion
  57.1 4.1 fusion.45
  61.3 1.6 copy-done.16
  63.2 2.1 split.60
  67.2 9.1 %fusion.44 = (f32[4,1024]{1,0:T(4,128)S(1)}, f32[4,1024,1024]{1,2,0:T(8,128)}) fusion(f32[1024,4]{0,1:T(4,128)S(1)} %fusion.28, f32[4,64]{1,0:T(4,128)S(1)} %mul.509, f32[1024,4,32]{0,2,1:T(8,128)S(1)} %get-tuple-element.65, f32[1024,4,32]{0,2,1:T(8,128)S(1)} %get-tuple-element.64, f32[1024,4]{0,1:T(4,128)S(1)} %fusion.27, ...), kind=kOutput, calls=%fused_computation.166 | convolution fusion | flops 551546880 | bytes 19973120 | tf_op jit(solution)/shard_map/qhd,khd->hqk/dot_general | solution.py:573
  76.3 8.1 %fusion = f32[4,1024]{1,0:T(4,128)S(1)} fusion(f32[4,1024,1024]{1,2,0:T(8,128)} %get-tuple-element.97, f32[4,1024]{1,0:T(4,128)S(1)} %get-tuple-element.96), kind=kLoop, calls=%fused_computation.6 | loop fusion | flops 8384512 | bytes 16809984 | tf_op jit(solution)/shard_map/reduce_sum | solution.py:578
  84.4 7.5 %fusion.14 = bf16[4,64,1024]{2,1,0:T(8,128)(2,1)S(1)} fusion(bf16[1024,4,64]{0,2,1:T(8,128)(2,1)S(1)} %bitcast.149, f32[4,1024,1024]{1,2,0:T(8,128)} %get-tuple-element.97, f32[4,1024]{1,0:T(4,128)S(1)} %fusion, f32[4,1024]{1,0:T(4,128)S(1)} %get-tuple-element.96), kind=kOutput, calls=%fused_computation.48 | convolution fusion | flops 549715968 | bytes 17858560 | tf_op jit(solution)/shard_map/hqk,khd->qhd/dot_general | solution.py:580
  91.9 2.0 convolution_convert_fusion.3
  94.0 18.6 %tensor_scatter.4 = f32[2,128,1024]{2,1,0:T(8,128)} custom-call(bf16[2,4,128,1024]{3,2,1,0:T(8,128)(2,1)} %bitcast.143), custom_call_target="tpu_custom_call" | custom-call | bytes 40000000 | tf_op jit(solution)/shard_map/tensor_scatter/pallas_call | solution.py:186
  112.5 1.4 multiply_reduce_fusion.11
  114.5 1.8 multiply_reduce_fusion.10
  116.3 0.9 multiply_convert_fusion.7.x_ref
  117.3 17.1 %tensor_gather.3 = bf16[2,4,128,1024]{3,2,1,0:T(8,128)(2,1)} custom-call(bf16[2,128,1024]{2,1,0:T(8,128)(2,1)} %multiply_convert_fusion.7.x_ref), custom_call_target="tpu_custom_call" | custom-call | bytes 40000000 | tf_op jit(solution)/shard_map/tensor_gather/pallas_call | solution.py:109
  135.0 1.7 fusion.23
  136.7 7.0 %fusion.46 = f32[1024,2048]{1,0:T(8,128)S(1)} fusion(bf16[1024,1024]{1,0:T(8,128)(2,1)} %bitcast.151, bf16[1024,2048]{1,0:T(8,128)(2,1)} %all-gather.3.cloned.1.call-done), kind=kOutput, calls=%fused_computation.168 | convolution fusion | flops 4294967296 | bytes 14680064 | tf_op jit(solution)/shard_map/dot_general | solution.py:527
  143.7 3.3 copy-done.14
  147.0 2.5 multiply_convert_fusion.3
  149.5 24.4 %all-gather.5.cloned.1.call-done = bf16[1024,1024]{0,1:T(8,128)(2,1)} async-done(((bf16[128,1024]{0,1:T(8,128)(2,1)}), bf16[1024,1024]{0,1:T(8,128)(2,1)}) %all-gather.5.cloned.1.call-update) | async-done | bytes 2097168 | tf_op jit(solution)/shard_map/all_gather | solution.py:657
  173.9 5.9 %convolution_convert_fusion.2 = bf16[1024,1024]{1,0:T(8,128)(2,1)} fusion(bf16[1024,1024]{1,0:T(8,128)(2,1)} %multiply_convert_fusion.3, bf16[1024,1024]{0,1:T(8,128)(2,1)} %all-gather.5.cloned.1.call-done), kind=kOutput, calls=%fused_computation.30 | convolution fusion | flops 2148532224 | bytes 6291456 | tf_op jit(solution)/shard_map/dot_general | solution.py:535
  179.8 18.5 %tensor_scatter.5 = f32[2,128,1024]{2,1,0:T(8,128)} custom-call(bf16[2,4,128,1024]{3,2,1,0:T(8,128)(2,1)} %bitcast.159), custom_call_target="tpu_custom_call" | custom-call | bytes 40000000 | tf_op jit(solution)/shard_map/tensor_scatter/pallas_call | solution.py:186
  198.3 1.5 multiply_reduce_fusion.9
  199.8 1.8 fusion.15
  201.7 1.6 multiply_reduce_fusion.7
  203.3 1.4 fusion.16.x_ref
  204.7 17.4 %tensor_gather.4 = bf16[2,4,128,1024]{3,2,1,0:T(8,128)(2,1)} custom-call(bf16[2,128,1024]{2,1,0:T(8,128)(2,1)} %fusion.16.x_ref), custom_call_target="tpu_custom_call" | custom-call | bytes 40000000 | tf_op jit(solution)/shard_map/tensor_gather/pallas_call | solution.py:109
  222.2 6.0 %convolution_convert_fusion.1 = bf16[1024,1024]{1,0:T(8,128)(2,1)} fusion(bf16[1024,1024]{1,0:T(8,128)(2,1)} %bitcast.155, bf16[1024,1024]{1,0:T(8,128)(2,1)} %multiply_convert_fusion.3), kind=kOutput, calls=%fused_computation.29 | convolution fusion | flops 2148532224 | bytes 6291456 | tf_op jit(solution)/shard_map/dot_general | solution.py:531
  228.2 10.0 %multiply_reduce_fusion.1 = (f32[1024]{0:T(1024)}, f32[1024]{0:T(1024)}, f32[1024,1024]{1,0:T(8,128)S(1)}, bf16[1024,1024]{1,0:T(8,128)(2,1)S(1)}) fusion(f32[1024,2048]{1,0:T(8,128)} %copy-done.14, f32[1024]{0:T(1024)} %param.27, f32[1024]{0:T(1024)} %param.26, bf16[1024,1024]{1,0:T(8,128)(2,1)} %bitcast.156, ...), kind=kOutput, calls=%fused_computation.15 | convolution fusion | flops 2168453120 | bytes 18890752 | tf_op jit(solution)/shard_map/dot_general | solution.py:527
  238.8 3.1 copy-done.72
  241.9 5.8 %fusion.10 = bf16[1024,1024]{1,0:T(8,128)(2,1)} fusion(bf16[1024,2048]{1,0:T(8,128)(2,1)S(1)} %copy-done.72, bf16[1024,1024]{1,0:T(8,128)(2,1)S(1)} %multiply_convert_fusion.1, bf16[1024,1024]{1,0:T(8,128)(2,1)S(1)} %get-tuple-element.54), kind=kOutput, calls=%fused_computation.28 | convolution fusion | flops 4304404480 | bytes 10485760 | tf_op jit(solution)/shard_map/dot_general | solution.py:535
  247.7 18.6 %tensor_scatter.6 = f32[2,128,1024]{2,1,0:T(8,128)} custom-call(bf16[2,4,128,1024]{3,2,1,0:T(8,128)(2,1)} %bitcast.157), custom_call_target="tpu_custom_call" | custom-call | bytes 40000000 | tf_op jit(solution)/shard_map/tensor_scatter/pallas_call | solution.py:186
  266.3 2.9 multiply_reduce_fusion.3
  269.9 3.3 multiply_reduce_fusion.4
  274.7 1.4 collective-permute-start.1
  276.2 1.0 fusion.17.x_ref
  277.2 17.5 %tensor_gather.5 = bf16[2,4,128,1024]{3,2,1,0:T(8,128)(2,1)} custom-call(bf16[2,128,1024]{2,1,0:T(8,128)(2,1)} %fusion.17.x_ref), custom_call_target="tpu_custom_call" | custom-call | bytes 40000000 | tf_op jit(solution)/shard_map/tensor_gather/pallas_call | solution.py:109
  294.8 2.5 convolution_convert_fusion.7
  297.6 8.1 %convolution_convert_fusion = bf16[1024,2048]{1,0:T(8,128)(2,1)} fusion(bf16[1024,1024]{1,0:T(8,128)(2,1)S(1)} %bitcast.152, bf16[1024,1024]{1,0:T(8,128)(2,1)S(1)} %copy-done.24, bf16[1024,1024]{1,0:T(8,128)(2,1)} %copy-done.74), kind=kOutput, calls=%fused_computation.24 | convolution fusion | flops 4305453056 | bytes 10485760 | tf_op jit(solution)/shard_map/dot_general | solution.py:531
  305.8 1.0 copy-done.20
  306.8 14.9 %multiply_reduce_fusion = (f32[4,1024]{1,0:T(4,128)S(1)}, f32[4,1024,1024]{1,2,0:T(8,128)}) fusion(f32[4,1024,1024]{1,2,0:T(8,128)} %get-tuple-element.97, f32[4,1024]{1,0:T(4,128)S(1)} %copy-done.40, bf16[1024,4,64]{0,2,1:T(8,128)(2,1)S(1)} %bitcast.147, bf16[1024,4,64]{0,2,1:T(8,128)(2,1)S(1)} %bitcast.150), kind=kOutput, calls=%fused_computation.1 | convolution fusion | flops 549449728 | bytes 34635776 | tf_op jit(solution)/shard_map/qhd,khd->hqk/dot_general | solution.py:596
  322.2 11.0 %multiply_convert_fusion = bf16[4,1024,1024]{1,2,0:T(8,128)(2,1)} fusion(f32[4,1024,1024]{1,2,0:T(8,128)} %get-tuple-element.99, f32[4,1024,1024]{1,2,0:T(8,128)S(1)} %bitcast.142, f32[4,1024]{1,0:T(4,128)S(1)} %get-tuple-element.98, f32[4,1024]{1,0:T(4,128)S(1)} %copy-done.40), kind=kLoop, calls=%fused_computation | loop fusion | flops 16777216 | bytes 41975808 | tf_op jit(solution)/shard_map/convert_element_type | solution.py:598
  333.3 6.3 %fusion.38 = f32[4,64,1024]{2,1,0:T(8,128)S(1)} fusion(bf16[4,1024,1024]{1,2,0:T(8,128)(2,1)} %multiply_convert_fusion, f32[4,64]{1,0:T(4,128)S(1)} %copy-done.47, f32[1024,4]{0,1:T(4,128)S(1)} %fusion.27, f32[1024,4,32]{0,2,1:T(8,128)S(1)} %copy-done.6, f32[1024,4,32]{0,2,1:T(8,128)S(1)} %copy-done.8), kind=kOutput, calls=%fused_computation.161 | convolution fusion | flops 537919488 | bytes 10503168 | tf_op jit(solution)/shard_map/hqk,qhd->khd/dot_general | solution.py:600
  339.6 3.1 fusion.19
  342.8 2.1 add_add_fusion.1
  346.0 8.8 %fusion.11 = bf16[4,64,1024]{2,1,0:T(8,128)(2,1)S(1)} fusion(bf16[1024,4,64]{0,2,1:T(8,128)(2,1)S(1)} %bitcast.148, f32[4,1024,1024]{1,2,0:T(8,128)} %get-tuple-element.97, f32[4,1024]{1,0:T(4,128)S(1)} %copy-done.40), kind=kOutput, calls=%fused_computation.45 | convolution fusion | flops 545521664 | bytes 17842176 | tf_op jit(solution)/shard_map/hqk,qhd->khd/dot_general | solution.py:595
  354.8 3.2 convolution_convert_fusion.4
  358.1 18.5 %tensor_scatter.7 = f32[2,128,1024]{2,1,0:T(8,128)} custom-call(bf16[2,4,128,1024]{3,2,1,0:T(8,128)(2,1)} %bitcast.158), custom_call_target="tpu_custom_call" | custom-call | bytes 40000000 | tf_op jit(solution)/shard_map/tensor_scatter/pallas_call | solution.py:186
  376.6 1.8 convolution_convert_fusion.6
  378.4 3.6 convolution_convert_fusion.5
  382.1 1.5 pad_maximum_fusion.3
  383.6 4.2 copy.35
  388.5 1.0 add_convert_fusion.input_ref
  389.6 1.0 fusion.25
  391.7 59.0 %sum_grads.1 = (bf16[2,128,1024]{2,1,0:T(8,128)(2,1)}, f32[4,40,128]{2,1,0:T(8,128)}, bf16[2,128,1024]{2,1,0:T(8,128)(2,1)}, bf16[2,128,2048]{2,1,0:T(8,128)(2,1)}, bf16[2,128,1024]{2,1,0:T(8,128)(2,1)}) custom-call(bf16[4,2,128,1024]{3,2,1,0:T(8,128)(2,1)} %bitcast.144, f32[40,128]{1,0:T(8,128)} %pad_bitcast_fusion.v_ref, ...), custom_call_target="tpu_custom_call" | custom-call | bytes 120000000 | tf_op jit(solution)/shard_map/sum_grads/pallas_call | solution.py:458
  450.7 1.0 copy.55
  454.1 2.1 convert_element_type.186
  456.2 1.2 bitcast_convert_fusion.2
  457.5 0.9 fusion.43
  459.4 1.3 copy.37
  461.0 1.5 fusion.42
  (217 shorter events, 16.7 us)
Async XLA Ops:
  7.2 47.6 %copy-start.71 = (f32[256]{0:T(256)S(1)}, f32[256]{0:T(256)}, u32[]{:S(2)}) copy-start(f32[256]{0:T(256)} %param.21) | copy-start | bytes 3076
  7.2 48.3 %copy-start.70 = (s32[2,1024]{1,0:T(2,128)S(1)}, s32[2,1024]{1,0:T(2,128)}, u32[]{:S(2)}) copy-start(s32[2,1024]{1,0:T(2,128)} %param.29) | copy-start | bytes 24580
  7.2 129.5 %all-gather.3.cloned.1.call-start = ((), (), s32[]{:S(2)}) async-start(), calls=%async_computation.2 | async-start | bytes 4718592 | tf_op jit(solution)/shard_map/all_gather | solution.py:656
  50.2 123.7 %all-gather.5.cloned.1.call-start = ((), (), s32[]{:S(2)}) async-start(), calls=%async_computation.3 | async-start | bytes 2359296 | tf_op jit(solution)/shard_map/all_gather | solution.py:657
  51.0 14.2 %collective-permute-start = (s32[512]{0:T(512)S(1)}, s32[512]{0:T(512)S(1)}, u32[]{:S(2)}, u32[]{:S(2)}) collective-permute-start(s32[512]{0:T(512)S(1)} %bitcast.183), channel_id=1, source_target_pairs={{0,4},{4,0},{1,5},{5,1},{2,6},{6,2},{3,7},{7,3},{8,12},{12,8},{9,1... | collective-permute-start | bytes 6152 | tf_op jit(solution)/shard_map/ppermute | solution.py:553
  53.2 81.8 %collective-permute-start.2 = (bf16[128,1024]{1,0:T(8,128)(2,1)}, bf16[128,1024]{1,0:T(8,128)(2,1)}, u32[]{:S(2)}, u32[]{:S(2)}) collective-permute-start(bf16[128,1024]{1,0:T(8,128)(2,1)} %dynamic-slice_bitcast_fusion), channel_id=1, source_target_pairs={{0,4},{4,0},{1,5},{5,1},{2,6},{6,2},{3,7},{7,3},{8,12},{12,8},{9,1... | collective-permute-start | bytes 786440 | tf_op jit(solution)/shard_map/ppermute | solution.py:553
  54.7 336.6 %reduce-scatter.3.cloned.1.call-start = ((), (), s32[]{:S(2)}) async-start(), calls=%async_computation.4 | async-start | bytes 2359296 | tf_op jit(solution)/shard_map/reduce_scatter | solution.py:722
  54.9 12.3 %copy-start.46 = (f32[4,64]{1,0:T(4,128)}, f32[4,64]{1,0:T(4,128)S(1)}, u32[]{:S(2)}) copy-start(f32[4,64]{1,0:T(4,128)S(1)} %mul.509) | copy-start | bytes 3076
  65.8 10.5 %copy-start.27 = (f32[1024,32]{0,1:T(8,128)}, f32[1024,32]{0,1:T(8,128)S(1)}, u32[]{:S(2)}) copy-start(f32[1024,32]{0,1:T(8,128)S(1)} %get-tuple-element.85) | copy-start | bytes 393220
  66.2 10.1 %copy-start.5 = (f32[1024,4,32]{0,2,1:T(8,128)}, f32[1024,4,32]{0,2,1:T(8,128)S(1)}, u32[]{:S(2)}) copy-start(f32[1024,4,32]{0,2,1:T(8,128)S(1)} %get-tuple-element.78) | copy-start | bytes 1572868
  66.2 10.1 %copy-start.7 = (f32[1024,4,32]{0,2,1:T(8,128)}, f32[1024,4,32]{0,2,1:T(8,128)S(1)}, u32[]{:S(2)}) copy-start(f32[1024,4,32]{0,2,1:T(8,128)S(1)} %get-tuple-element.79) | copy-start | bytes 1572868
  66.5 9.8 %copy-start.43 = (f32[1024,4]{0,1:T(4,128)}, f32[1024,4]{0,1:T(4,128)S(1)}, u32[]{:S(2)}) copy-start(f32[1024,4]{0,1:T(4,128)S(1)} %get-tuple-element.101) | copy-start | bytes 49156
  67.1 9.2 %copy-start.30 = (f32[1024,4]{0,1:T(4,128)}, f32[1024,4]{0,1:T(4,128)S(1)}, u32[]{:S(2)}) copy-start(f32[1024,4]{0,1:T(4,128)S(1)} %fusion.28) | copy-start | bytes 49156
  76.3 8.1 %copy-start.19 = (bf16[1024,256]{0,1:T(8,128)(2,1)S(1)}, bf16[1024,256]{0,1:T(8,128)(2,1)}, u32[]{:S(2)}) copy-start(bf16[1024,256]{0,1:T(8,128)(2,1)} %split.60) | copy-start | bytes 1572868
  84.4 7.5 %copy-start.37 = (bf16[256,1024]{1,0:T(8,128)(2,1)S(1)}, bf16[256,1024]{1,0:T(8,128)(2,1)}, u32[]{:S(2)}) copy-start(bf16[256,1024]{1,0:T(8,128)(2,1)} %get-tuple-element.28) | copy-start | bytes 1572868
  91.9 22.6 %copy-start.49 = (f32[1024]{0:T(1024)S(1)}, f32[1024]{0:T(1024)}, u32[]{:S(2)}) copy-start(f32[1024]{0:T(1024)} %param.22) | copy-start | bytes 12292
  112.5 22.5 %copy-start.32 = (bf16[2,128,1024]{2,1,0:T(8,128)(2,1)S(1)}, bf16[2,128,1024]{2,1,0:T(8,128)(2,1)}, u32[]{:S(2)}) copy-start(bf16[2,128,1024]{2,1,0:T(8,128)(2,1)} %param.31) | copy-start | bytes 1572868
  116.3 18.7 %copy-start.64 = (f32[2,128]{1,0:T(2,128)}, f32[2,128]{1,0:T(2,128)S(1)}, u32[]{:S(2)}) copy-start(f32[2,128]{1,0:T(2,128)S(1)} %get-tuple-element.52) | copy-start | bytes 3076
  116.3 18.7 %copy-start.52 = (f32[2,128]{1,0:T(2,128)}, f32[2,128]{1,0:T(2,128)S(1)}, u32[]{:S(2)}) copy-start(f32[2,128]{1,0:T(2,128)S(1)} %fusion.31) | copy-start | bytes 3076
  136.7 10.3 %copy-start.59 = (f32[1024]{0:T(1024)S(1)}, f32[1024]{0:T(1024)}, u32[]{:S(2)}) copy-start(f32[1024]{0:T(1024)} %param.27) | copy-start | bytes 12292
  136.7 10.3 %copy-start.67 = (f32[1024]{0:T(1024)S(1)}, f32[1024]{0:T(1024)}, u32[]{:S(2)}) copy-start(f32[1024]{0:T(1024)} %param.26) | copy-start | bytes 12292
  198.3 3.4 copy-start.3
  198.3 5.0 %copy-start.9 = (bf16[1,128,1024]{2,1,0:T(8,128)(2,1)S(1)}, bf16[1,128,1024]{2,1,0:T(8,128)(2,1)}, u32[]{:S(2)}) copy-start(bf16[1,128,1024]{2,1,0:T(8,128)(2,1)} %get-tuple-element.75) | copy-start | bytes 786436
  198.3 5.0 %copy-start.45 = (f32[1024]{0:T(1024)S(1)}, f32[1024]{0:T(1024)}, u32[]{:S(2)}) copy-start(f32[1024]{0:T(1024)} %param.28) | copy-start | bytes 12292
  198.3 5.0 %copy-start.53 = (f32[2,128]{1,0:T(2,128)S(1)}, f32[2,128]{1,0:T(2,128)}, u32[]{:S(2)}) copy-start(f32[2,128]{1,0:T(2,128)} %copy-done.52) | copy-start | bytes 3076
  199.8 3.4 copy-start.54
  228.2 163.5 %reduce-scatter.5.cloned.1.call-start = ((), (), s32[]{:S(2)}) async-start(), calls=%async_computation.5 | async-start | bytes 4718592 | tf_op jit(solution)/shard_map/reduce_scatter | solution.py:722
  228.2 10.0 %copy-start.60 = (f32[1024]{0:T(1024)S(1)}, f32[1024]{0:T(1024)}, u32[]{:S(2)}) copy-start(f32[1024]{0:T(1024)} %param.27) | copy-start | bytes 12292
  238.2 9.5 %copy-start.74 = (bf16[1024,1024]{1,0:T(8,128)(2,1)}, bf16[1024,1024]{1,0:T(8,128)(2,1)S(1)}, u32[]{:S(2)}) copy-start(bf16[1024,1024]{1,0:T(8,128)(2,1)S(1)} %get-tuple-element.54) | copy-start | bytes 6291460
  238.2 3.7 copy-start.72
  238.8 8.9 %copy-start.23 = (bf16[1024,1024]{1,0:T(8,128)(2,1)}, bf16[1024,1024]{1,0:T(8,128)(2,1)S(1)}, u32[]{:S(2)}) copy-start(bf16[1024,1024]{1,0:T(8,128)(2,1)S(1)} %multiply_convert_fusion.1) | copy-start | bytes 6291460
  266.3 3.6 copy-start.11
  269.2 7.0 %copy-start.66 = (f32[2,128]{1,0:T(2,128)S(1)}, f32[2,128]{1,0:T(2,128)}, u32[]{:S(2)}) copy-start(f32[2,128]{1,0:T(2,128)} %copy-done.65) | copy-start | bytes 3076
  269.2 7.0 %copy-start.4 = (f32[2,128,1024]{2,1,0:T(8,128)S(1)}, f32[2,128,1024]{2,1,0:T(8,128)}, u32[]{:S(2)}) copy-start(f32[2,128,1024]{2,1,0:T(8,128)} %tensor_scatter.4) | copy-start | bytes 3145732
  269.2 7.0 %copy-start.50 = (f32[1024]{0:T(1024)S(1)}, f32[1024]{0:T(1024)}, u32[]{:S(2)}) copy-start(f32[1024]{0:T(1024)} %param.22) | copy-start | bytes 12292
  269.2 7.0 %copy-start.62 = (f32[2,128]{1,0:T(2,128)S(1)}, f32[2,128]{1,0:T(2,128)}, u32[]{:S(2)}) copy-start(f32[2,128]{1,0:T(2,128)} %copy-done.61) | copy-start | bytes 3076
  273.2 21.6 %copy-start.38 = (bf16[256,1024]{1,0:T(8,128)(2,1)S(1)}, bf16[256,1024]{1,0:T(8,128)(2,1)}, u32[]{:S(2)}) copy-start(bf16[256,1024]{1,0:T(8,128)(2,1)} %get-tuple-element.28) | copy-start | bytes 1572868
  274.7 114.8 %collective-permute-start.1 = (bf16[128,1024]{1,0:T(8,128)(2,1)}, bf16[128,1024]{1,0:T(8,128)(2,1)}, u32[]{:S(2)}, u32[]{:S(2)}) collective-permute-start(bf16[128,1024]{1,0:T(8,128)(2,1)} %dynamic-slice_bitcast_fusion.1), channel_id=1, source_target_pairs={{0,4},{4,0},{1,5},{5,1},{2,6},{6,2},{3,7},{7,3},{8,12},{12,8},{9,1... | collective-permute-start | bytes 786440 | tf_op jit(solution)/shard_map/ppermute | solution.py:553
  297.6 8.1 %copy-start.17 = (bf16[1024,256]{0,1:T(8,128)(2,1)}, bf16[1024,256]{0,1:T(8,128)(2,1)S(1)}, u32[]{:S(2)}) copy-start(bf16[1024,256]{0,1:T(8,128)(2,1)S(1)} %convolution_convert_fusion.7) | copy-start | bytes 1572868
  305.8 15.9 %slice-start = ((s8[16777216]{0:T(1024)(128)(4,1)}), s8[4194304]{0:T(1024)(128)(4,1)S(1)}, s32[]{:S(2)}) async-start(s8[16777216]{0:T(1024)(128)(4,1)} %bitcast.141), calls=%async_computation.6 | async-start | bytes 8388608
  306.8 14.9 %slice-start.1 = ((s8[16777216]{0:T(1024)(128)(4,1)}), s8[4194304]{0:T(1024)(128)(4,1)S(1)}, s32[]{:S(2)}) async-start(s8[16777216]{0:T(1024)(128)(4,1)} %bitcast.141), calls=%async_computation.7 | async-start | bytes 8388608
  306.8 14.9 %slice-start.2 = ((s8[16777216]{0:T(1024)(128)(4,1)}), s8[4194304]{0:T(1024)(128)(4,1)S(1)}, s32[]{:S(2)}) async-start(s8[16777216]{0:T(1024)(128)(4,1)} %bitcast.141), calls=%async_computation.8 | async-start | bytes 8388608
  306.8 15.4 %slice-start.3 = ((s8[16777216]{0:T(1024)(128)(4,1)}), s8[4194304]{0:T(1024)(128)(4,1)S(1)}, s32[]{:S(2)}) async-start(s8[16777216]{0:T(1024)(128)(4,1)} %bitcast.141), calls=%async_computation.9 | async-start | bytes 8388608
  322.2 11.0 %copy-start.6 = (f32[1024,4,32]{0,2,1:T(8,128)S(1)}, f32[1024,4,32]{0,2,1:T(8,128)}, u32[]{:S(2)}) copy-start(f32[1024,4,32]{0,2,1:T(8,128)} %copy-done.5) | copy-start | bytes 1572868
  322.2 11.0 %copy-start.8 = (f32[1024,4,32]{0,2,1:T(8,128)S(1)}, f32[1024,4,32]{0,2,1:T(8,128)}, u32[]{:S(2)}) copy-start(f32[1024,4,32]{0,2,1:T(8,128)} %copy-done.7) | copy-start | bytes 1572868
  322.2 11.0 %copy-start.47 = (f32[4,64]{1,0:T(4,128)S(1)}, f32[4,64]{1,0:T(4,128)}, u32[]{:S(2)}) copy-start(f32[4,64]{1,0:T(4,128)} %copy-done.46) | copy-start | bytes 3076
  333.2 6.3 %copy-start.2 = (bf16[4,1024,1024]{1,2,0:T(8,128)(2,1)S(1)}, bf16[4,1024,1024]{1,2,0:T(8,128)(2,1)}, u32[]{:S(2)}) copy-start(bf16[4,1024,1024]{1,2,0:T(8,128)(2,1)} %multiply_convert_fusion) | copy-start | bytes 25165828
  333.2 6.3 %copy-start.31 = (f32[1024,4]{0,1:T(4,128)S(1)}, f32[1024,4]{0,1:T(4,128)}, u32[]{:S(2)}) copy-start(f32[1024,4]{0,1:T(4,128)} %copy-done.30) | copy-start | bytes 49156
  333.2 6.3 %copy-start.48 = (f32[4,64]{1,0:T(4,128)S(1)}, f32[4,64]{1,0:T(4,128)}, u32[]{:S(2)}) copy-start(f32[4,64]{1,0:T(4,128)} %broadcast_multiply_fusion) | copy-start | bytes 3076
  346.0 8.8 %copy-start.34 = (bf16[1024,4,64]{0,2,1:T(8,128)(2,1)}, bf16[1024,4,64]{0,2,1:T(8,128)(2,1)S(1)}, u32[]{:S(2)}) copy-start(bf16[1024,4,64]{0,2,1:T(8,128)(2,1)S(1)} %add_convert_fusion.1) | copy-start | bytes 1572868
  346.0 8.8 %copy-start.73 = (bf16[4,256,768]{2,1,0:T(8,128)(2,1)S(1)}, bf16[4,256,768]{2,1,0:T(8,128)(2,1)}, u32[]{:S(2)}) copy-start(bf16[4,256,768]{2,1,0:T(8,128)(2,1)} %get-tuple-element.27) | copy-start | bytes 4718596
  354.8 21.8 %copy-start.22 = (bf16[2,4,128,1024]{3,2,1,0:T(8,128)(2,1)S(1)}, bf16[2,4,128,1024]{3,2,1,0:T(8,128)(2,1)}, u32[]{:S(2)}) copy-start(bf16[2,4,128,1024]{3,2,1,0:T(8,128)(2,1)} %tensor_gather.5) | copy-start | bytes 6291460
  358.0 20.3 %copy-start.35 = (bf16[1024,4,64]{0,2,1:T(8,128)(2,1)S(1)}, bf16[1024,4,64]{0,2,1:T(8,128)(2,1)}, u32[]{:S(2)}) copy-start(bf16[1024,4,64]{0,2,1:T(8,128)(2,1)} %copy-done.34) | copy-start | bytes 1572868
  382.0 5.8 %copy-start.57 = (f32[4352]{0:T(1024)S(1)}, f32[4352]{0:T(1024)}, u32[]{:S(2)}) copy-start(f32[4352]{0:T(1024)} %custom-call) | copy-start | bytes 52228
  382.0 5.8 %copy-start.69 = (f32[1024]{0:T(1024)S(1)}, f32[1024]{0:T(1024)}, u32[]{:S(2)}) copy-start(f32[1024]{0:T(1024)} %get-tuple-element.37) | copy-start | bytes 12292
  382.0 5.8 %copy-start.68 = (f32[1024]{0:T(1024)S(1)}, f32[1024]{0:T(1024)}, u32[]{:S(2)}) copy-start(f32[1024]{0:T(1024)} %get-tuple-element.36) | copy-start | bytes 12292
  382.0 5.9 %copy-start.63 = (f32[1024]{0:T(1024)S(1)}, f32[1024]{0:T(1024)}, u32[]{:S(2)}) copy-start(f32[1024]{0:T(1024)} %get-tuple-element.42) | copy-start | bytes 12292
  382.0 5.9 %copy-start.58 = (f32[1024]{0:T(1024)S(1)}, f32[1024]{0:T(1024)}, u32[]{:S(2)}) copy-start(f32[1024]{0:T(1024)} %get-tuple-element.38) | copy-start | bytes 12292
  382.0 6.5 %copy-start.13 = (f32[2,128,1024]{2,1,0:T(8,128)S(1)}, f32[2,128,1024]{2,1,0:T(8,128)}, u32[]{:S(2)}) copy-start(f32[2,128,1024]{2,1,0:T(8,128)} %copy-done.12) | copy-start | bytes 3145732
  382.0 6.5 %copy-start.15 = (f32[2,128,1024]{2,1,0:T(8,128)S(1)}, f32[2,128,1024]{2,1,0:T(8,128)}, u32[]{:S(2)}) copy-start(f32[2,128,1024]{2,1,0:T(8,128)} %tensor_scatter.7) | copy-start | bytes 3145732
  382.0 6.5 %copy-start.51 = (f32[1024]{0:T(1024)S(1)}, f32[1024]{0:T(1024)}, u32[]{:S(2)}) copy-start(f32[1024]{0:T(1024)} %param.22) | copy-start | bytes 12292
  383.6 6.0 %copy-start.26 = (bf16[2,128,1024]{2,1,0:T(8,128)(2,1)S(1)}, bf16[2,128,1024]{2,1,0:T(8,128)(2,1)}, u32[]{:S(2)}) copy-start(bf16[2,128,1024]{2,1,0:T(8,128)(2,1)} %copy-done.25) | copy-start | bytes 1572868
  450.7 8.5 %copy-start.33 = (bf16[2,128,1024]{2,1,0:T(8,128)(2,1)S(1)}, bf16[2,128,1024]{2,1,0:T(8,128)(2,1)}, u32[]{:S(2)}) copy-start(bf16[2,128,1024]{2,1,0:T(8,128)(2,1)} %get-tuple-element.35) | copy-start | bytes 1572868
  456.2 4.5 copy-start.29
  (22 other events, 44.7 us)
Sparse Core Ops, SparseCore 0:
  50.3 71.9 all-gather.2
  124.9 48.9 all-gather.4
  228.3 66.2 reduce-scatter.2
  305.9 85.7 reduce-scatter.4
where the time goes:
time: 474 us; the launch traced here: 469 us
  Pallas kernels  225 us (47%)
  matrix products  110 us (23%)
  other arithmetic  59.6 us (13%)
  local copies, waits for them, and re-layouts  32 us (7%)
  waiting for transfers between devices  24.8 us (5%)
  between operations  15.2 us (3%)
    pallas_call x4, Pallas kernels, tensor_scatter(): pl.pallas_call(functools.partial(scatter_kernel, chunks), out_shape=jax.S...  74.1 us
    pallas_call x1, Pallas kernels, sum_grads(): pl.pallas_call(functools.partial(grads_kernel, n), out_shape=(jax.ShapeDt...  59 us
    pallas_call x3, Pallas kernels, tensor_gather(): pl.pallas_call(functools.partial(gather_kernel, chunks), out_shape=jax.Sh...  52.1 us
    pallas_call x1, Pallas kernels, opening(): pl.pallas_call(functools.partial(opening_kernel, n), out_shape=(jax.Shape...  39.3 us
    all_gather x1, waiting for transfers between devices, run(): full_down = lax.all_gather(down_half, ('fsdp', 'ctx'), axis=0, tiled=True)  24.4 us
    dot_general x4, matrix products, product(): return jnp.dot(left, right, preferred_element_type=F32)  23.1 us
    dot_general x4, matrix products, transposed_left(): lax.dot_general(left, right, (((0,), (0,)), ((), ())), preferred_element_...  19.4 us
    dot_general x4, matrix products, transposed_right(): lax.dot_general(left, right, (((1,), (1,)), ((), ())), preferred_element_...  17.4 us
  transfers between devices with their start and end apart: 7, of which 2 were waited for; matrix products, arithmetic and copies ran while one was open for 33% of the time, Pallas kernels for 19%

commit v1 on v0

--- a/solution.py
+++ b/solution.py
@@ -52,9 +52,224 @@
     return [(h, pl.ds(i * step, step)) for h in range(halves) for i in range(parts)]
 
 
-def gather_kernel(chunks, x_ref, out_ref, local_sem, send, receive):
+class Rider:
+    arrays = ()
+    shapes = ()
+    scratch = ()
+    remote_copies = 0
+    local_copies = 0
+
+    def place(self):
+        ctx = lax.axis_index("ctx")
+        z = lax.axis_index("fsdp")
+        return ctx, 1 - ctx, z
+
+    def finish_copies(self, copies, own):
+        for copy in copies:
+            copy.wait_recv()
+        for copy in copies:
+            copy.wait_send()
+        for copy in own:
+            copy.wait()
+
+
+class Spread(Rider):
+    def __init__(self, n, half):
+        self.n = n
+        self.arrays = (half,)
+        self.shapes = (jax.ShapeDtypeStruct((n,) + half.shape, half.dtype),)
+        self.remote_copies = n - 1
+        self.local_copies = 1
+
+    def peers(self):
+        _, _, z = self.place()
+        return [{"fsdp": lax.rem(z + d, self.n)} for d in range(1, self.n)]
+
+    def start(self, inputs, outputs, scratch, send, receive, local):
+        _, _, z = self.place()
+        own = [pltpu.make_async_copy(inputs[0], outputs[0].at[z], local.at[0])]
+        copies = [
+            remote(inputs[0], outputs[0].at[z], send.at[i], receive.at[i], **where)
+            for i, where in enumerate(self.peers())
+        ]
+        for copy in copies + own:
+            copy.start()
+        return lambda: self.finish_copies(copies, own)
+
+
+class Hand(Rider):
+    def __init__(self, n, halves, rest):
+        self.n = n
+        self.arrays = (halves, rest)
+        self.shapes = (jax.ShapeDtypeStruct((n, 2) + rest.shape, rest.dtype),)
+        self.remote_copies = n - 1
+        self.local_copies = 2
+
+    def peers(self):
+        return [{"ctx": self.place()[1]}]
+
+    def start(self, inputs, outputs, scratch, send, receive, local):
+        ctx, other, z = self.place()
+        halves, rest = inputs
+        full = outputs[0]
+        copies = []
+        for d in range(1, self.n):
+            block = lax.rem(z + d, self.n)
+            copies.append(
+                remote(
+                    halves.at[block],
+                    full.at[block, ctx],
+                    send.at[d - 1],
+                    receive.at[d - 1],
+                    ctx=other,
+                )
+            )
+        own = [
+            pltpu.make_async_copy(halves, full.at[:, ctx], local.at[0]),
+            pltpu.make_async_copy(rest, full.at[z, other], local.at[1]),
+        ]
+        for copy in copies + own:
+            copy.start()
+        return lambda: self.finish_copies(copies, own)
+
+
+class Near(Rider):
+    def __init__(self, n, partial):
+        self.n = n
+        block = (n,) + partial.shape[2:]
+        self.arrays = (partial,)
+        self.shapes = (jax.ShapeDtypeStruct(block, BF),)
+        self.scratch = (pltpu.VMEM(block, BF),)
+        self.remote_copies = n
+
+    def peers(self):
+        return [{"ctx": self.place()[1]}]
+
+    def start(self, inputs, outputs, scratch, send, receive, local):
+        ctx, other, _ = self.place()
+        partial, out, arrived = inputs[0], outputs[0], scratch[0]
+        copies = [
+            remote(partial.at[i, other], arrived.at[i], send.at[i], receive.at[i], ctx=other)
+            for i in range(self.n)
+        ]
+        for copy in copies:
+            copy.start()
+
+        def finish():
+            for i, copy in enumerate(copies):
+                copy.wait_recv()
+                out[i] = (partial[i, ctx].astype(F32) + arrived[i].astype(F32)).astype(BF)
+            for copy in copies:
+                copy.wait_send()
+
+        return finish
+
+
+class Line(Rider):
+    def __init__(self, n, terms):
+        self.n = n
+        self.arrays = (terms,)
+        self.shapes = (jax.ShapeDtypeStruct(terms.shape[1:], BF),)
+        self.scratch = (pltpu.VMEM((n,) + terms.shape[1:], BF),)
+        self.remote_copies = n - 1
+
+    def peers(self):
+        _, _, z = self.place()
+        return [{"fsdp": lax.rem(z + d, self.n)} for d in range(1, self.n)]
+
+    def start(self, inputs, outputs, scratch, send, receive, local):
+        _, _, z = self.place()
+        terms, out, far = inputs[0], outputs[0], scratch[0]
+        copies = []
+        for d in range(1, self.n):
+            block = lax.rem(z + d, self.n)
+            copies.append(
+                remote(
+                    terms.at[block], far.at[d], send.at[d - 1], receive.at[d - 1], fsdp=block
+                )
+            )
+            copies[-1].start()
+
+        def finish():
+            total = terms[z].astype(F32)
+            for d in range(1, self.n):
+                copies[d - 1].wait_recv()
+                total = total + far[d].astype(F32)
+            out[...] = total.astype(BF)
+            for copy in copies:
+                copy.wait_send()
+
+        return finish
+
+
+class Swap(Rider):
+    def __init__(self, share):
+        self.arrays = (share,)
+        self.shapes = (jax.ShapeDtypeStruct((2,) + share.shape, share.dtype),)
+        self.remote_copies = 1
+        self.local_copies = 1
+
+    def peers(self):
+        return [{"ctx": self.place()[1]}]
+
+    def start(self, inputs, outputs, scratch, send, receive, local):
+        ctx, other, _ = self.place()
+        copies = [remote(inputs[0], outputs[0].at[ctx], send.at[0], receive.at[0], ctx=other)]
+        own = [pltpu.make_async_copy(inputs[0], outputs[0].at[ctx], local.at[0])]
+        for copy in copies + own:
+            copy.start()
+        return lambda: self.finish_copies(copies, own)
+
+
+def with_rider(body, rider, own_scratch, *refs):
+    if rider is None:
+        body([], lambda: (lambda: None), *refs)
+        return
+    sizes = [1, len(rider.arrays), 1, len(rider.shapes), own_scratch, len(rider.scratch), 3]
+    groups = []
+    start = 0
+    for size in sizes:
+        groups.append(refs[start : start + size])
+        start += size
+    x, inputs, out, outputs, scratch, extra, semaphores = groups
+
+    def launch():
+        return rider.start(inputs, outputs, extra, *semaphores)
+
+    body(rider.peers(), launch, *x, *out, *scratch)
+
+
+def call_tensor(body, array, shape, scratch, rider, number, name):
+    own_scratch = len(scratch)
+    arrays, shapes = [array], [shape]
+    if rider is not None:
+        arrays += rider.arrays
+        shapes += rider.shapes
+        scratch = (
+            list(scratch)
+            + list(rider.scratch)
+            + [
+                pltpu.SemaphoreType.DMA((rider.remote_copies,)),
+                pltpu.SemaphoreType.DMA((rider.remote_copies,)),
+                pltpu.SemaphoreType.DMA((max(rider.local_copies, 1),)),
+            ]
+        )
+    result = pl.pallas_call(
+        functools.partial(with_rider, body, rider, own_scratch),
+        out_shape=tuple(shapes),
+        in_specs=[IN_VMEM] * len(arrays),
+        out_specs=(IN_VMEM,) * len(shapes),
+        scratch_shapes=scratch,
+        compiler_params=pltpu.CompilerParams(collective_id=number, has_side_effects=True),
+        cost_estimate=pl.CostEstimate(flops=0, bytes_accessed=40_000_000, transcendentals=0),
+        name=name,
+    )(*arrays)
+    return result[0] if rider is None else result
+
+
+def gather_kernel(chunks, peers, launch, x_ref, out_ref, local_sem, send, receive):
     me, partner, across, _ = tensor_peers()
-    meet([{"tp": partner}, {"tp": across}])
+    meet([{"tp": partner}, {"tp": across}] + peers)
     own = pltpu.make_async_copy(x_ref, out_ref.at[:, me], local_sem)
     own.start()
     count = len(chunks)
@@ -81,6 +296,7 @@
             )
         )
         side[-1].start()
+    finish = launch()
     for i, (h, rows) in enumerate(chunks):
         over[i].wait_recv()
         relay.append(
@@ -101,30 +317,32 @@
         side[i].wait_send()
         relay[i].wait_send()
     own.wait()
-
-
-def tensor_gather(values):
+    finish()
+
+
+def tensor_gather(values, rider=None, number=0):
     halves, rows, width = values.shape
     chunks = row_chunks(halves, rows, 2)
-    return pl.pallas_call(
+    return call_tensor(
         functools.partial(gather_kernel, chunks),
-        out_shape=jax.ShapeDtypeStruct((halves, 4, rows, width), values.dtype),
-        in_specs=[IN_VMEM],
-        out_specs=IN_VMEM,
-        scratch_shapes=[
+        values,
+        jax.ShapeDtypeStruct((halves, 4, rows, width), values.dtype),
+        [
             pltpu.SemaphoreType.DMA,
             pltpu.SemaphoreType.DMA((3 * len(chunks),)),
             pltpu.SemaphoreType.DMA((3 * len(chunks),)),
         ],
-        compiler_params=pltpu.CompilerParams(collective_id=0, has_side_effects=True),
-        cost_estimate=pl.CostEstimate(flops=0, bytes_accessed=40_000_000, transcendentals=0),
-        name="tensor_gather",
-    )(values)
-
-
-def scatter_kernel(chunks, p_ref, out_ref, pair, mine, far, joined, send, receive):
+        rider,
+        number,
+        "tensor_gather",
+    )
+
+
+def scatter_kernel(
+    chunks, peers, launch, p_ref, out_ref, pair, mine, far, joined, send, receive
+):
     me, partner, across, diagonal = tensor_peers()
-    meet([{"tp": partner}, {"tp": across}])
+    meet([{"tp": partner}, {"tp": across}] + peers)
     count = len(chunks)
     first, second, third = [], [], []
     for i, (h, rows) in enumerate(chunks):
@@ -149,6 +367,7 @@
             )
         )
         second[-1].start()
+    finish = launch()
     for i, (h, rows) in enumerate(chunks):
         first[i].wait_recv()
         joined[h, rows] = (
@@ -177,26 +396,26 @@
         first[i].wait_send()
         second[i].wait_send()
         third[i].wait_send()
-
-
-def tensor_scatter(partial):
+    finish()
+
+
+def tensor_scatter(partial, rider=None, number=1):
     halves, _, rows, width = partial.shape
     chunks = row_chunks(halves, rows, 2)
     block = pltpu.VMEM((halves, rows, width), BF)
-    return pl.pallas_call(
+    return call_tensor(
         functools.partial(scatter_kernel, chunks),
-        out_shape=jax.ShapeDtypeStruct((halves, rows, width), F32),
-        in_specs=[IN_VMEM],
-        out_specs=IN_VMEM,
-        scratch_shapes=[block] * 4
+        partial,
+        jax.ShapeDtypeStruct((halves, rows, width), F32),
+        [block] * 4
         + [
             pltpu.SemaphoreType.DMA((3 * len(chunks),)),
             pltpu.SemaphoreType.DMA((3 * len(chunks),)),
         ],
-        compiler_params=pltpu.CompilerParams(collective_id=1, has_side_effects=True),
-        cost_estimate=pl.CostEstimate(flops=0, bytes_accessed=40_000_000, transcendentals=0),
-        name="tensor_scatter",
-    )(partial)
+        rider,
+        number,
+        "tensor_scatter",
+    )
 
 
 def opening_kernel(
@@ -334,12 +553,10 @@
     n,
     g_ref,
     v_ref,
-    down_ref,
     ug_ref,
     input_ref,
     out_ref,
     sums_ref,
-    full_down_ref,
     full_ug_ref,
     traded_ref,
     arrived,
@@ -379,13 +596,11 @@
         near[d].start()
     shares = [
         remote(input_ref.at[other], traded_ref.at[ctx], share_send.at[0], share_receive.at[0], ctx=other),
-        remote(down_ref, full_down_ref.at[ctx], share_send.at[1], share_receive.at[1], ctx=other),
-        remote(ug_ref, full_ug_ref.at[ctx], share_send.at[2], share_receive.at[2], ctx=other),
+        remote(ug_ref, full_ug_ref.at[ctx], share_send.at[1], share_receive.at[1], ctx=other),
     ]
     own = [
         pltpu.make_async_copy(input_ref.at[ctx], traded_ref.at[ctx], local.at[0]),
-        pltpu.make_async_copy(down_ref, full_down_ref.at[ctx], local.at[1]),
-        pltpu.make_async_copy(ug_ref, full_ug_ref.at[ctx], local.at[2]),
+        pltpu.make_async_copy(ug_ref, full_ug_ref.at[ctx], local.at[1]),
     ]
     for copy in shares + own:
         copy.start()
@@ -451,21 +666,20 @@
     last.wait_send()
 
 
-def sum_grads(n, parts, vectors, down_share, ug_share, traded):
+def sum_grads(n, parts, vectors, ug_share, traded):
     total_rows, width = parts.shape
     rows = total_rows // (2 * n)
     vector = pltpu.VMEM(vectors.shape, F32)
-    out, sums, down, ug, traded = pl.pallas_call(
+    out, sums, ug, traded = pl.pallas_call(
         functools.partial(grads_kernel, n),
         out_shape=(
             jax.ShapeDtypeStruct((2, rows, width), BF),
             jax.ShapeDtypeStruct((4,) + vectors.shape, F32),
-            jax.ShapeDtypeStruct((2,) + down_share.shape, BF),
             jax.ShapeDtypeStruct((2,) + ug_share.shape, BF),
             jax.ShapeDtypeStruct(traded.shape, BF),
         ),
-        in_specs=[IN_VMEM] * 5,
-        out_specs=(IN_VMEM,) * 5,
+        in_specs=[IN_VMEM] * 4,
+        out_specs=(IN_VMEM,) * 4,
         scratch_shapes=[
             pltpu.VMEM((n, rows, width), BF),
             pltpu.VMEM((n, rows, width), BF),
@@ -478,18 +692,17 @@
             pltpu.SemaphoreType.DMA((2 * n,)),
             pltpu.SemaphoreType.DMA((n + 3,)),
             pltpu.SemaphoreType.DMA((n + 3,)),
-            pltpu.SemaphoreType.DMA((3,)),
-            pltpu.SemaphoreType.DMA((3,)),
-            pltpu.SemaphoreType.DMA((3,)),
+            pltpu.SemaphoreType.DMA((2,)),
+            pltpu.SemaphoreType.DMA((2,)),
+            pltpu.SemaphoreType.DMA((2,)),
         ],
         compiler_params=pltpu.CompilerParams(collective_id=3, has_side_effects=True),
         cost_estimate=pl.CostEstimate(flops=0, bytes_accessed=120_000_000, transcendentals=0),
         name="sum_grads",
-    )(parts.reshape(n, 2, rows, width), vectors, down_share, ug_share, traded)
+    )(parts.reshape(n, 2, rows, width), vectors, ug_share, traded)
     return (
         out.reshape(2 * rows, width),
         sums,
-        down.reshape(-1, down.shape[2]),
         ug.reshape(-1, ug.shape[2]),
         traded,
     )
@@ -634,17 +847,17 @@
 
         ctx = lax.axis_index("ctx")
 
-        def own_half(shard):
+        def half_of(shard, index):
             half = shard.shape[0] // 2
-            return lax.dynamic_slice_in_dim(shard, ctx * half, half, 0)
-
-        ug_half = own_half(jnp.concatenate([up_weight, gate_weight], axis=1))
-        down_half = own_half(down_weight.T)
+            return lax.dynamic_slice_in_dim(shard, index * half, half, 0)
+
+        ug_half = half_of(jnp.concatenate([up_weight, gate_weight], axis=1), ctx)
+        down_half = half_of(down_weight.T, ctx)
         if small:
             gathered, full_qkv, full_output = opening(
                 n, residual, query_weight, key_weight, value_weight, output_weight
             )
-            gathered, ug_half, down_half = lax.optimization_barrier((gathered, ug_half, down_half))
+            gathered, ug_half = lax.optimization_barrier((gathered, ug_half))
             tensor_index = lax.axis_index("tp")
             mine = lax.dynamic_index_in_dim(gathered, tensor_index, 1, keepdims=False)
         else:
@@ -654,7 +867,8 @@
             full_output = lax.all_gather(output_weight, "fsdp", axis=1, tiled=True)
             gathered = tensor_gather(mine)
         full_ug = lax.all_gather(ug_half, ("fsdp", "ctx"), axis=0, tiled=True)
-        full_down = lax.all_gather(down_half, ("fsdp", "ctx"), axis=0, tiled=True)
+        if not small:
+            full_down = lax.all_gather(down_half, ("fsdp", "ctx"), axis=0, tiled=True)
 
         ids = lax.dynamic_index_in_dim(block_ids, ctx, 0, keepdims=False)
         my_positions = trade(positions, sizes).reshape(-1)
@@ -674,16 +888,26 @@
         value_low = raw_value.astype(BF)
         attended, logsum = attend_both(query_low, key_low, value_low, ids)
 
-        def reduce_rows(partial):
-            return tensor_scatter(partial.astype(BF).reshape(shape4))
-
-        def gather_rows(values):
-            return tensor_gather(values.astype(BF)).reshape(-1, width)
-
-        attend_sum = reduce_rows(product(attended, full_output))
+        def reduce_rows(partial, *rider):
+            return tensor_scatter(partial.astype(BF).reshape(shape4), *rider)
+
+        def gather_rows(values, *rider):
+            return tensor_gather(values.astype(BF), *rider)
+
+        partial = product(attended, full_output)
+        if small:
+            attend_sum, down_halves = reduce_rows(partial, Spread(n, down_half), 5)
+        else:
+            attend_sum = reduce_rows(partial)
         residual_float = mine.astype(F32)
         first, attend_back_mix = jax.vjp(branch_mix, attend_sum, residual_float, attend_rate)
-        first_all = gather_rows(first)
+        if small:
+            down_rest = half_of(down_weight.T, 1 - ctx)
+            first_all, full_down = gather_rows(first, Hand(n, down_halves, down_rest), 6)
+            full_down = full_down.reshape(width, hidden_here)
+        else:
+            first_all = gather_rows(first)
+        first_all = first_all.reshape(-1, width)
         ug_raw = product(first_all, full_ug)
         up_raw, gate_raw = ug_raw[:, :hidden_here], ug_raw[:, hidden_here:]
         hidden, activate_back = jax.vjp(activate, up_raw, gate_raw, amplitude, steepness)
@@ -693,17 +917,27 @@
         layer_out = trade(outcome.astype(BF), sizes)
         my_cot = trade(cotangent, sizes)
         grad_down_sum, grad_first, grad_mixer_part = mixer_back(my_cot.astype(F32))
-        down_grad_all = gather_rows(grad_down_sum)
+        down_grad_all = gather_rows(grad_down_sum).reshape(-1, width)
         grad_hidden = product(down_grad_all, full_down)
         grad_down_part = transposed_left(down_grad_all, hidden_low)
         grad_up_raw, grad_gate_raw, grad_amplitude_part, grad_steepness_part = activate_back(
             grad_hidden
         )
         ug_grad = jnp.concatenate([grad_up_raw.astype(BF), grad_gate_raw.astype(BF)], axis=1)
-        grad_first = grad_first + reduce_rows(transposed_right(ug_grad, full_ug))
         grad_ug_part = transposed_left(first_all, ug_grad)
+        partial = transposed_right(ug_grad, full_ug)
+        if small:
+            terms = grad_down_part.astype(BF).reshape(n, 2, -1, hidden_here)
+            summed, down_terms = reduce_rows(partial, Near(n, terms), 7)
+        else:
+            summed = reduce_rows(partial)
+        grad_first = grad_first + summed
         grad_attend_sum, grad_residual, grad_attend_part = attend_back_mix(grad_first)
-        attend_grad_all = gather_rows(grad_attend_sum)
+        if small:
+            attend_grad_all, down_share = gather_rows(grad_attend_sum, Line(n, down_terms), 8)
+        else:
+            attend_grad_all = gather_rows(grad_attend_sum)
+        attend_grad_all = attend_grad_all.reshape(-1, width)
         grad_output_part = transposed_left(attend_grad_all, attended)
         grad_attended = transposed_right(attend_grad_all, full_output).astype(BF)
         grad_query_ready, grad_key_ready, grad_value_ready = attend_back(
@@ -714,7 +948,13 @@
         qkv_grad = jnp.concatenate(
             [grad_raw_query.astype(BF), grad_raw_key.astype(BF), grad_value_ready.astype(BF)], axis=1
         )
-        grad_input = grad_residual + reduce_rows(transposed_right(qkv_grad, full_qkv))
+        partial = transposed_right(qkv_grad, full_qkv)
+        if small:
+            summed, grad_down = reduce_rows(partial, Swap(down_share), 9)
+            grad_down = grad_down.reshape(-1, hidden_here)
+        else:
+            summed = reduce_rows(partial)
+        grad_input = grad_residual + summed
         grad_input = grad_input.astype(BF)
         grad_qkv_part = transposed_left(flat_in, qkv_grad)
 
@@ -733,17 +973,14 @@
         lengths = [vector.shape[0] for vector in vectors]
         packed = jnp.concatenate(vectors)
         packed = jnp.pad(packed, (0, -packed.shape[0] % 1024)).reshape(-1, 128)
-        down_share = scatter_rows(grad_down_part)
         ug_share = scatter_rows(grad_ug_part)
         late = jnp.concatenate([grad_qkv_part.astype(BF), grad_output_part.astype(BF)], axis=1)
         if small:
-            late, sums, grad_down, grad_ug, grad_input = sum_grads(
-                n, late, packed, down_share, ug_share, grad_input
-            )
+            late, sums, grad_ug, grad_input = sum_grads(n, late, packed, ug_share, grad_input)
         else:
             late = swap_halves(scatter_rows(late), ctx)
             sums = lax.all_gather(lax.psum(packed, ("fsdp", "ctx")), "tp", axis=0)
-            grad_down = swap_halves(down_share, ctx)
+            grad_down = swap_halves(scatter_rows(grad_down_part), ctx)
             grad_ug = swap_halves(ug_share, ctx)
             grad_input = trade(grad_input, sizes)
         late = late.astype(F32)

time: 474 us -> 512 us (1.080)
  Pallas kernels: 225 us -> 298 us
  waiting for transfers between devices: 24.8 us -> 0.06 us
    pallas_call x7, Pallas kernels: 126 us -> 188 us  [call_tensor(): pl.pallas_call(functools.partial(with_rider, body, rider, own_scratch), o...]
    all_gather x1 -> x0, waiting for transfers between devices: 24.4 us -> none  [run(): full_down = lax.all_gather(down_half, ('fsdp', 'ctx'), axis=0, tiled=True)]
    pallas_call x1, Pallas kernels: 59 us -> 72 us  [sum_grads(): pl.pallas_call(functools.partial(grads_kernel, n), out_shape=(jax.ShapeDt...]
    dot_general x4, matrix products: 19.4 us -> 12.9 us  [transposed_left(): lax.dot_general(left, right, (((0,), (0,)), ((), ())), preferred_element_...]
    unnamed x169 -> x167, local copies, waits for them, and re-layouts: 17.2 us -> 15.1 us
  transfers between devices with their start and end apart: 7 -> 5, of which waited for: 2 -> 0; matrix products, arithmetic and copies ran while one was open for 33% -> 26% of each run, Pallas kernels for 19% -> 38%
where the time goes in v1:
time: 512 us; the launch traced here: 508 us
  Pallas kernels  298 us (58%)
  matrix products  106 us (21%)
  other arithmetic  56.6 us (11%)
  local copies, waits for them, and re-layouts  27.4 us (5%)
  between operations  15.5 us (3%)
    pallas_call x7, Pallas kernels, call_tensor(): pl.pallas_call(functools.partial(with_rider, body, rider, own_scratch), o...  188 us
    pallas_call x1, Pallas kernels, sum_grads(): pl.pallas_call(functools.partial(grads_kernel, n), out_shape=(jax.ShapeDt...  72 us
    pallas_call x1, Pallas kernels, opening(): pl.pallas_call(functools.partial(opening_kernel, n), out_shape=(jax.Shape...  37.8 us
    dot_general x4, matrix products, product(): return jnp.dot(left, right, preferred_element_type=F32)  23 us
    dot_general x4, matrix products, transposed_right(): lax.dot_general(left, right, (((1,), (1,)), ((), ())), preferred_element_...  20.2 us
    dot_general x1, matrix products, attend_back(): grad_w = jnp.einsum('qhd,khd->hqk', g, v, preferred_element_type=F32)  15.3 us
    unnamed x167, local copies, waits for them, and re-layouts  15.1 us
    dot_general x4, matrix products, transposed_left(): lax.dot_general(left, right, (((0,), (0,)), ((), ())), preferred_element_...  12.9 us
  transfers between devices with their start and end apart: 5, of which 0 were waited for; matrix products, arithmetic and copies ran while one was open for 26% of the time, Pallas kernels for 38%

profile of v1, /device:TPU:0, one launch (start us, length us, event | category | flops | bytes accessed | tf_op | source)
XLA Modules:
  0.0 507.5 jit_solution(7634249911295696612)
XLA Ops:
  8.0 3.0 collective-permute-start
  11.0 1.0 dynamic-slice_bitcast_fusion
  12.0 1.9 fusion.22
  13.9 37.8 %opening.1 = (bf16[2,4,128,1024]{3,2,1,0:T(8,128)(2,1)}, bf16[4,256,768]{2,1,0:T(8,128)(2,1)}, bf16[256,1024]{1,0:T(8,128)(2,1)}) custom-call(bf16[2,128,1024]{2,1,0:T(8,128)(2,1)} %x_ref.1, bf16[256,256]{1,0:T(8,128)(2,1)} %q_ref.1, bf16[256,256]{1,0:T(8,128)(2,1)} %k_ref.1, bf16[256,256]{1,0:T(8,128)(2,1)} %v_ref.1, bf16[256,256]{1,0:T(8,128)(2,1)} %o_ref.1), custom_call_target="tpu_custom_call" | custom-call | bytes 60000000 | tf_op jit(solution)/shard_map/opening/pallas_call | solution.py:531
  52.6 1.6 broadcast_compare_fusion
  54.2 3.9 fusion.45
  58.1 1.6 copy-done.18
  60.9 1.3 split.60
  62.2 0.9 copy.45
  63.1 0.9 copy.44
  65.2 0.9 copy-done.46
  66.1 8.3 %fusion.44 = (f32[4,1024]{1,0:T(4,128)S(1)}, f32[4,1024,1024]{1,2,0:T(8,128)}) fusion(f32[1024,4]{0,1:T(4,128)S(1)} %fusion.28, f32[4,64]{1,0:T(4,128)S(1)} %mul.512, f32[1024,4,32]{0,2,1:T(8,128)S(1)} %get-tuple-element.81, f32[1024,4,32]{0,2,1:T(8,128)S(1)} %get-tuple-element.80, f32[1024,4]{0,1:T(4,128)S(1)} %fusion.27, ...), kind=kOutput, calls=%fused_computation.167 | convolution fusion | flops 551546880 | bytes 19973120 | tf_op jit(solution)/shard_map/qhd,khd->hqk/dot_general | solution.py:786
  74.5 8.0 %fusion = f32[4,1024]{1,0:T(4,128)S(1)} fusion(f32[4,1024,1024]{1,2,0:T(8,128)} %get-tuple-element.115, f32[4,1024]{1,0:T(4,128)S(1)} %get-tuple-element.114), kind=kLoop, calls=%fused_computation.6 | loop fusion | flops 8384512 | bytes 16809984 | tf_op jit(solution)/shard_map/reduce_sum | solution.py:791
  82.5 8.0 %fusion.14 = bf16[4,64,1024]{2,1,0:T(8,128)(2,1)S(1)} fusion(bf16[1024,4,64]{0,2,1:T(8,128)(2,1)S(1)} %bitcast.151, f32[4,1024,1024]{1,2,0:T(8,128)} %get-tuple-element.115, f32[4,1024]{1,0:T(4,128)S(1)} %fusion, f32[4,1024]{1,0:T(4,128)S(1)} %get-tuple-element.114), kind=kOutput, calls=%fused_computation.48 | convolution fusion | flops 549715968 | bytes 17858560 | tf_op jit(solution)/shard_map/hqk,khd->qhd/dot_general | solution.py:793
  90.5 2.1 convolution_convert_fusion.3
  92.6 39.4 %tensor_scatter.4 = (f32[2,128,1024]{2,1,0:T(8,128)}, bf16[4,128,1024]{2,1,0:T(8,128)(2,1)}) custom-call(bf16[2,4,128,1024]{3,2,1,0:T(8,128)(2,1)} %bitcast.145, bf16[128,1024]{1,0:T(8,128)(2,1)} %bitcast.160), custom_call_target="tpu_custom_call" | custom-call | bytes 40000000 | tf_op jit(solution)/shard_map/tensor_scatter/pallas_call | solution.py:257
  132.1 1.4 multiply_reduce_fusion.11
  133.5 1.8 multiply_reduce_fusion.10
  135.3 0.9 multiply_convert_fusion.7.refs_0_
  136.3 22.6 %tensor_gather.3 = (bf16[2,4,128,1024]{3,2,1,0:T(8,128)(2,1)}, bf16[4,2,128,1024]{3,2,1,0:T(8,128)(2,1)}) custom-call(bf16[2,128,1024]{2,1,0:T(8,128)(2,1)} %multiply_convert_fusion.7.refs_0_, bf16[4,128,1024]{2,1,0:T(8,128)(2,1)} %get-tuple-element.38.refs_1_, bf16[128,1024]{1,0:T(8,128)(2,1)} %bitcast.159), custom_call_target="tpu_custom_call" | custom-call | bytes 40000000 | tf_op jit(solution)/shard_map/tensor_gather/pallas_call | solution.py:257
  159.5 1.0 fusion.23
  160.6 7.0 %fusion.46 = f32[1024,2048]{1,0:T(8,128)S(1)} fusion(bf16[1024,1024]{1,0:T(8,128)(2,1)} %bitcast.187, bf16[1024,2048]{1,0:T(8,128)(2,1)} %all-gather.2.cloned.1.call-done), kind=kOutput, calls=%fused_computation.169 | convolution fusion | flops 4294967296 | bytes 14680064 | tf_op jit(solution)/shard_map/dot_general | solution.py:740
  167.6 1.5 multiply_convert_fusion.3
  169.2 2.0 copy-done.16
  171.2 3.7 convolution_convert_fusion.2
  174.9 18.5 %tensor_scatter.5 = f32[2,128,1024]{2,1,0:T(8,128)} custom-call(bf16[2,4,128,1024]{3,2,1,0:T(8,128)(2,1)} %bitcast.156), custom_call_target="tpu_custom_call" | custom-call | bytes 40000000 | tf_op jit(solution)/shard_map/tensor_scatter/pallas_call | solution.py:257
  193.5 1.5 multiply_reduce_fusion.9
  194.9 1.8 fusion.15
  197.5 1.4 fusion.16.refs_0_
  198.9 17.4 %tensor_gather.4 = bf16[2,4,128,1024]{3,2,1,0:T(8,128)(2,1)} custom-call(bf16[2,128,1024]{2,1,0:T(8,128)(2,1)} %fusion.16.refs_0_), custom_call_target="tpu_custom_call" | custom-call | bytes 40000000 | tf_op jit(solution)/shard_map/tensor_gather/pallas_call | solution.py:257
  216.3 10.0 %multiply_reduce_fusion.1 = (f32[1024]{0:T(1024)}, f32[1024]{0:T(1024)}, f32[1024,1024]{1,0:T(8,128)S(1)}, bf16[1024,1024]{1,0:T(8,128)(2,1)S(1)}) fusion(f32[1024,2048]{1,0:T(8,128)} %copy-done.16, f32[1024]{0:T(1024)S(1)} %copy-done.58, f32[1024]{0:T(1024)S(1)} %copy-done.65, bf16[1024,1024]{1,0:T(8,128)(2,1)} %bitcast.153, bf16[1024,1024]{1,0:T(8,128)(2,1)} %bitcast.189), kind=kOutput, calls=%fused_computation.15 | convolution fusion | flops 2168453120 | bytes 18890752 | tf_op jit(solution)/shard_map/dot_general | solution.py:740
  226.3 3.8 convolution_convert_fusion.1
  230.7 1.3 copy-done.26
  232.1 6.7 %convolution_convert_fusion = bf16[1024,2048]{1,0:T(8,128)(2,1)} fusion(bf16[1024,1024]{1,0:T(8,128)(2,1)S(1)} %bitcast.188, bf16[1024,1024]{1,0:T(8,128)(2,1)S(1)} %multiply_convert_fusion.1, bf16[1024,1024]{1,0:T(8,128)(2,1)S(1)} %get-tuple-element.70), kind=kOutput, calls=%fused_computation.24 | convolution fusion | flops 4305453056 | bytes 10485760 | tf_op jit(solution)/shard_map/dot_general | solution.py:744
  238.8 9.4 %fusion.10 = bf16[1024,1024]{1,0:T(8,128)(2,1)} fusion(bf16[1024,2048]{1,0:T(8,128)(2,1)} %all-gather.2.cloned.1.call-done, bf16[1024,1024]{1,0:T(8,128)(2,1)} %copy-done.26, bf16[1024,1024]{1,0:T(8,128)(2,1)} %copy-done.72), kind=kOutput, calls=%fused_computation.28 | convolution fusion | flops 4304404480 | bytes 10485760 | tf_op jit(solution)/shard_map/dot_general | solution.py:748
  248.1 40.9 %tensor_scatter.6 = (f32[2,128,1024]{2,1,0:T(8,128)}, bf16[4,128,1024]{2,1,0:T(8,128)(2,1)}) custom-call(bf16[2,4,128,1024]{3,2,1,0:T(8,128)(2,1)} %bitcast.158, bf16[4,2,128,1024]{3,2,1,0:T(8,128)(2,1)} %bitcast.157), custom_call_target="tpu_custom_call" | custom-call | bytes 40000000 | tf_op jit(solution)/shard_map/tensor_scatter/pallas_call | solution.py:257
  289.0 2.9 multiply_reduce_fusion.3
  292.6 3.1 multiply_reduce_fusion.4
  296.5 0.9 collective-permute-start.1
  297.4 1.0 fusion.17.refs_0_
  298.4 32.0 %tensor_gather.5 = (bf16[2,4,128,1024]{3,2,1,0:T(8,128)(2,1)}, bf16[128,1024]{1,0:T(8,128)(2,1)}) custom-call(bf16[2,128,1024]{2,1,0:T(8,128)(2,1)} %fusion.17.refs_0_, bf16[4,128,1024]{2,1,0:T(8,128)(2,1)} %get-tuple-element.43.refs_1_), custom_call_target="tpu_custom_call" | custom-call | bytes 40000000 | tf_op jit(solution)/shard_map/tensor_gather/pallas_call | solution.py:257
  330.5 2.3 convolution_convert_fusion.7
  332.9 15.3 %multiply_reduce_fusion = (f32[4,1024]{1,0:T(4,128)S(1)}, f32[4,1024,1024]{1,2,0:T(8,128)}) fusion(f32[4,1024,1024]{1,2,0:T(8,128)} %get-tuple-element.115, f32[4,1024]{1,0:T(4,128)S(1)} %copy-done.45, bf16[1024,4,64]{0,2,1:T(8,128)(2,1)S(1)} %bitcast.149, bf16[1024,4,64]{0,2,1:T(8,128)(2,1)S(1)} %bitcast.152), kind=kOutput, calls=%fused_computation.1 | convolution fusion | flops 549449728 | bytes 34635776 | tf_op jit(solution)/shard_map/qhd,khd->hqk/dot_general | solution.py:809
  348.2 1.4 slice-done.3
  349.6 11.0 %multiply_convert_fusion = bf16[4,1024,1024]{1,2,0:T(8,128)(2,1)} fusion(f32[4,1024,1024]{1,2,0:T(8,128)} %get-tuple-element.117, f32[4,1024,1024]{1,2,0:T(8,128)S(1)} %bitcast.144, f32[4,1024]{1,0:T(4,128)S(1)} %get-tuple-element.116, f32[4,1024]{1,0:T(4,128)S(1)} %copy-done.45), kind=kLoop, calls=%fused_computation | loop fusion | flops 16777216 | bytes 41975808 | tf_op jit(solution)/shard_map/convert_element_type | solution.py:811
  360.7 6.2 %fusion.38 = f32[4,64,1024]{2,1,0:T(8,128)S(1)} fusion(bf16[4,1024,1024]{1,2,0:T(8,128)(2,1)} %multiply_convert_fusion, f32[4,64]{1,0:T(4,128)S(1)} %mul.512, f32[1024,4]{0,1:T(4,128)S(1)} %copy-done.34, f32[1024,4,32]{0,2,1:T(8,128)S(1)} %copy-done.10, f32[1024,4,32]{0,2,1:T(8,128)S(1)} %copy-done.12), kind=kOutput, calls=%fused_computation.162 | convolution fusion | flops 537919488 | bytes 10503168 | tf_op jit(solution)/shard_map/hqk,qhd->khd/dot_general | solution.py:813
  367.0 3.2 fusion.19
  370.9 1.8 add_add_fusion.1
  375.2 8.6 %fusion.11 = bf16[4,64,1024]{2,1,0:T(8,128)(2,1)S(1)} fusion(bf16[1024,4,64]{0,2,1:T(8,128)(2,1)S(1)} %bitcast.150, f32[4,1024,1024]{1,2,0:T(8,128)} %get-tuple-element.115, f32[4,1024]{1,0:T(4,128)S(1)} %copy-done.45), kind=kOutput, calls=%fused_computation.45 | convolution fusion | flops 545521664 | bytes 17842176 | tf_op jit(solution)/shard_map/hqk,qhd->khd/dot_general | solution.py:808
  383.8 1.8 convolution_convert_fusion.5
  385.9 2.6 copy.37
  388.5 4.8 convolution_convert_fusion.4
  393.3 17.7 %tensor_scatter.7 = (f32[2,128,1024]{2,1,0:T(8,128)}, bf16[2,128,1024]{2,1,0:T(8,128)(2,1)}) custom-call(bf16[2,4,128,1024]{3,2,1,0:T(8,128)(2,1)} %bitcast.155, bf16[128,1024]{1,0:T(8,128)(2,1)} %get-tuple-element.45.refs_1_), custom_call_target="tpu_custom_call" | custom-call | bytes 40000000 | tf_op jit(solution)/shard_map/tensor_scatter/pallas_call | solution.py:257
  411.0 1.1 bitcast_convert_fusion.1
  412.1 1.3 copy.39
  414.2 2.3 add_convert_fusion.input_ref
  416.4 1.0 fusion.25
  417.5 0.8 pad_maximum_fusion.11
  418.3 72.0 %sum_grads.1 = (bf16[2,128,1024]{2,1,0:T(8,128)(2,1)}, f32[4,40,128]{2,1,0:T(8,128)}, bf16[2,128,2048]{2,1,0:T(8,128)(2,1)}, bf16[2,128,1024]{2,1,0:T(8,128)(2,1)}) custom-call(bf16[4,2,128,1024]{3,2,1,0:T(8,128)(2,1)} %bitcast.146, f32[40,128]{1,0:T(8,128)} %pad_bitcast_fusion.v_ref, bf16[128,2048]{1,0:T(8,128)(2,1)} %reduce-scatter.2.cloned.1.call-done.ug_ref, ...), custom_call_target="tpu_custom_call" | custom-call | bytes 120000000 | tf_op jit(solution)/shard_map/sum_grads/pallas_call | solution.py:673
  490.3 1.0 copy.59
  493.7 2.1 convert_element_type.186
  495.8 1.1 bitcast_convert_fusion.2
  497.0 0.9 fusion.43
  499.0 1.5 fusion.42
  (209 shorter events, 15.2 us)
Async XLA Ops:
  7.2 45.4 %copy-start = (s32[2,1024]{1,0:T(2,128)S(1)}, s32[2,1024]{1,0:T(2,128)}, u32[]{:S(2)}) copy-start(s32[2,1024]{1,0:T(2,128)} %param.29) | copy-start | bytes 24580
  7.2 153.4 %all-gather.2.cloned.1.call-start = ((), (), s32[]{:S(2)}) async-start(), calls=%async_computation.1 | async-start | bytes 4718592 | tf_op jit(solution)/shard_map/all_gather | solution.py:869
  8.0 55.9 %collective-permute-start = (s32[512]{0:T(512)S(1)}, s32[512]{0:T(512)S(1)}, u32[]{:S(2)}, u32[]{:S(2)}) collective-permute-start(s32[512]{0:T(512)S(1)} %bitcast.184), channel_id=1, source_target_pairs={{0,4},{4,0},{1,5},{5,1},{2,6},{6,2},{3,7},{7,3},{8,12},{12,8},{9,1... | collective-permute-start | bytes 6152 | tf_op jit(solution)/shard_map/ppermute | solution.py:766
  12.0 147.5 %collective-permute-start.2 = (bf16[128,1024]{1,0:T(8,128)(2,1)S(1)}, bf16[128,1024]{1,0:T(8,128)(2,1)}, u32[]{:S(2)}, u32[]{:S(2)}) collective-permute-start(bf16[128,1024]{1,0:T(8,128)(2,1)S(1)} %dynamic-slice_bitcast_fusion), channel_id=1, source_target_pairs={{0,4},{4,0},{1,5},{5,1},{2,6},{6,2},{3,7},{7,3},{8,12},{12,8},{9,1... | collective-permute-start | bytes 786440 | tf_op jit(solution)/shard_map/ppermute | solution.py:766
  51.8 366.5 %reduce-scatter.2.cloned.1.call-start = ((), (), s32[]{:S(2)}) async-start(), calls=%async_computation.2 | async-start | bytes 4718592 | tf_op jit(solution)/shard_map/reduce_scatter | solution.py:962
  62.2 20.3 %copy-start.21 = (bf16[1024,256]{0,1:T(8,128)(2,1)}, bf16[1024,256]{0,1:T(8,128)(2,1)S(1)}, u32[]{:S(2)}) copy-start(bf16[1024,256]{0,1:T(8,128)(2,1)S(1)} %split.60) | copy-start | bytes 1572868
  64.5 9.9 %copy-start.29 = (f32[1024,32]{0,1:T(8,128)}, f32[1024,32]{0,1:T(8,128)S(1)}, u32[]{:S(2)}) copy-start(f32[1024,32]{0,1:T(8,128)S(1)} %get-tuple-element.103) | copy-start | bytes 393220
  64.8 9.6 %copy-start.5 = (f32[1024,4,32]{0,2,1:T(8,128)}, f32[1024,4,32]{0,2,1:T(8,128)S(1)}, u32[]{:S(2)}) copy-start(f32[1024,4,32]{0,2,1:T(8,128)S(1)} %get-tuple-element.80) | copy-start | bytes 1572868
  64.8 9.6 %copy-start.7 = (f32[1024,4,32]{0,2,1:T(8,128)}, f32[1024,4,32]{0,2,1:T(8,128)S(1)}, u32[]{:S(2)}) copy-start(f32[1024,4,32]{0,2,1:T(8,128)S(1)} %get-tuple-element.81) | copy-start | bytes 1572868
  64.8 9.6 %copy-start.9 = (f32[1024,4,32]{0,2,1:T(8,128)}, f32[1024,4,32]{0,2,1:T(8,128)S(1)}, u32[]{:S(2)}) copy-start(f32[1024,4,32]{0,2,1:T(8,128)S(1)} %get-tuple-element.96) | copy-start | bytes 1572868
  64.8 9.6 %copy-start.11 = (f32[1024,4,32]{0,2,1:T(8,128)}, f32[1024,4,32]{0,2,1:T(8,128)S(1)}, u32[]{:S(2)}) copy-start(f32[1024,4,32]{0,2,1:T(8,128)S(1)} %get-tuple-element.97) | copy-start | bytes 1572868
  65.1 9.3 %copy-start.48 = (f32[1024,4]{0,1:T(4,128)}, f32[1024,4]{0,1:T(4,128)S(1)}, u32[]{:S(2)}) copy-start(f32[1024,4]{0,1:T(4,128)S(1)} %get-tuple-element.119) | copy-start | bytes 49156
  66.1 8.3 %copy-start.33 = (f32[1024,4]{0,1:T(4,128)}, f32[1024,4]{0,1:T(4,128)S(1)}, u32[]{:S(2)}) copy-start(f32[1024,4]{0,1:T(4,128)S(1)} %fusion.27) | copy-start | bytes 49156
  66.1 8.3 %copy-start.35 = (f32[1024,4]{0,1:T(4,128)}, f32[1024,4]{0,1:T(4,128)S(1)}, u32[]{:S(2)}) copy-start(f32[1024,4]{0,1:T(4,128)S(1)} %fusion.28) | copy-start | bytes 49156
  82.5 8.0 %copy-start.41 = (bf16[256,1024]{1,0:T(8,128)(2,1)S(1)}, bf16[256,1024]{1,0:T(8,128)(2,1)}, u32[]{:S(2)}) copy-start(bf16[256,1024]{1,0:T(8,128)(2,1)} %get-tuple-element.36) | copy-start | bytes 1572868
  90.5 42.9 %copy-start.51 = (f32[1024]{0:T(1024)S(1)}, f32[1024]{0:T(1024)}, u32[]{:S(2)}) copy-start(f32[1024]{0:T(1024)} %param.22) | copy-start | bytes 12292
  92.6 66.9 %copy-start.37 = (bf16[2,128,1024]{2,1,0:T(8,128)(2,1)S(1)}, bf16[2,128,1024]{2,1,0:T(8,128)(2,1)}, u32[]{:S(2)}) copy-start(bf16[2,128,1024]{2,1,0:T(8,128)(2,1)} %param.31) | copy-start | bytes 1572868
  133.5 34.1 %copy-start.59 = (f32[2,128]{1,0:T(2,128)}, f32[2,128]{1,0:T(2,128)S(1)}, u32[]{:S(2)}) copy-start(f32[2,128]{1,0:T(2,128)S(1)} %fusion.30) | copy-start | bytes 3076
  135.3 32.3 %copy-start.62 = (f32[2,128]{1,0:T(2,128)}, f32[2,128]{1,0:T(2,128)S(1)}, u32[]{:S(2)}) copy-start(f32[2,128]{1,0:T(2,128)S(1)} %get-tuple-element.68) | copy-start | bytes 3076
  135.3 62.1 %copy-start.52 = (f32[2,128]{1,0:T(2,128)}, f32[2,128]{1,0:T(2,128)S(1)}, u32[]{:S(2)}) copy-start(f32[2,128]{1,0:T(2,128)S(1)} %fusion.31) | copy-start | bytes 3076
  160.5 36.9 %copy-start.13 = (bf16[1,128,1024]{2,1,0:T(8,128)(2,1)}, bf16[1,128,1024]{2,1,0:T(8,128)(2,1)S(1)}, u32[]{:S(2)}) copy-start(bf16[1,128,1024]{2,1,0:T(8,128)(2,1)S(1)} %get-tuple-element.91) | copy-start | bytes 786436
  160.6 7.1 %copy-start.58 = (f32[1024]{0:T(1024)S(1)}, f32[1024]{0:T(1024)}, u32[]{:S(2)}) copy-start(f32[1024]{0:T(1024)} %param.27) | copy-start | bytes 12292
  160.6 7.0 %copy-start.65 = (f32[1024]{0:T(1024)S(1)}, f32[1024]{0:T(1024)}, u32[]{:S(2)}) copy-start(f32[1024]{0:T(1024)} %param.26) | copy-start | bytes 12292
  167.6 3.5 copy-start.16
  171.2 3.7 copy-start.24
  174.9 20.0 %copy-start.50 = (f32[1024]{0:T(1024)S(1)}, f32[1024]{0:T(1024)}, u32[]{:S(2)}) copy-start(f32[1024]{0:T(1024)} %param.28) | copy-start | bytes 12292
  194.9 3.9 copy-start.53
  196.7 19.6 %copy-start.54 = (f32[2,128]{1,0:T(2,128)}, f32[2,128]{1,0:T(2,128)S(1)}, u32[]{:S(2)}) copy-start(f32[2,128]{1,0:T(2,128)S(1)} %get-tuple-element.112) | copy-start | bytes 3076
  196.7 19.6 %copy-start.55 = (f32[2,128]{1,0:T(2,128)}, f32[2,128]{1,0:T(2,128)S(1)}, u32[]{:S(2)}) copy-start(f32[2,128]{1,0:T(2,128)S(1)} %get-tuple-element.113) | copy-start | bytes 3076
  216.3 10.0 %copy-start.23 = (bf16[2,4,128,1024]{3,2,1,0:T(8,128)(2,1)S(1)}, bf16[2,4,128,1024]{3,2,1,0:T(8,128)(2,1)}, u32[]{:S(2)}) copy-start(bf16[2,4,128,1024]{3,2,1,0:T(8,128)(2,1)} %tensor_gather.4) | copy-start | bytes 6291460
  216.3 10.0 %copy-start.25 = (bf16[1024,1024]{1,0:T(8,128)(2,1)S(1)}, bf16[1024,1024]{1,0:T(8,128)(2,1)}, u32[]{:S(2)}) copy-start(bf16[1024,1024]{1,0:T(8,128)(2,1)} %copy-done.24) | copy-start | bytes 6291460
  226.3 4.4 copy-start.72
  248.1 44.5 %copy-start.4 = (f32[2,128,1024]{2,1,0:T(8,128)S(1)}, f32[2,128,1024]{2,1,0:T(8,128)}, u32[]{:S(2)}) copy-start(f32[2,128,1024]{2,1,0:T(8,128)} %get-tuple-element.37) | copy-start | bytes 3145732
  289.0 3.6 copy-start.17
  292.0 3.8 copy-start.64
  292.0 5.4 %copy-start.60 = (f32[2,128]{1,0:T(2,128)S(1)}, f32[2,128]{1,0:T(2,128)}, u32[]{:S(2)}) copy-start(f32[2,128]{1,0:T(2,128)} %copy-done.59) | copy-start | bytes 3076
  295.7 34.7 %copy-start.42 = (bf16[256,1024]{1,0:T(8,128)(2,1)S(1)}, bf16[256,1024]{1,0:T(8,128)(2,1)}, u32[]{:S(2)}) copy-start(bf16[256,1024]{1,0:T(8,128)(2,1)} %get-tuple-element.36) | copy-start | bytes 1572868
  296.5 120.0 %collective-permute-start.1 = (bf16[128,1024]{1,0:T(8,128)(2,1)}, bf16[128,1024]{1,0:T(8,128)(2,1)}, u32[]{:S(2)}, u32[]{:S(2)}) collective-permute-start(bf16[128,1024]{1,0:T(8,128)(2,1)} %dynamic-slice_bitcast_fusion.1), channel_id=1, source_target_pairs={{0,4},{4,0},{1,5},{5,1},{2,6},{6,2},{3,7},{7,3},{8,12},{12,8},{9,1... | collective-permute-start | bytes 786440 | tf_op jit(solution)/shard_map/ppermute | solution.py:766
  298.4 34.4 %copy-start.22 = (bf16[1024,256]{0,1:T(8,128)(2,1)S(1)}, bf16[1024,256]{0,1:T(8,128)(2,1)}, u32[]{:S(2)}) copy-start(bf16[1024,256]{0,1:T(8,128)(2,1)} %copy-done.21) | copy-start | bytes 1572868
  298.4 34.4 %copy-start.45 = (f32[4,1024]{1,0:T(4,128)S(1)}, f32[4,1024]{1,0:T(4,128)}, u32[]{:S(2)}) copy-start(f32[4,1024]{1,0:T(4,128)} %log_add_fusion) | copy-start | bytes 49156
  332.8 15.4 %copy-start.19 = (bf16[1024,256]{0,1:T(8,128)(2,1)}, bf16[1024,256]{0,1:T(8,128)(2,1)S(1)}, u32[]{:S(2)}) copy-start(bf16[1024,256]{0,1:T(8,128)(2,1)S(1)} %convolution_convert_fusion.7) | copy-start | bytes 1572868
  332.8 15.4 %slice-start = ((s8[16777216]{0:T(1024)(128)(4,1)}), s8[4194304]{0:T(1024)(128)(4,1)S(1)}, s32[]{:S(2)}) async-start(s8[16777216]{0:T(1024)(128)(4,1)} %bitcast.143), calls=%async_computation.3 | async-start | bytes 8388608
  332.8 15.3 %slice-start.1 = ((s8[16777216]{0:T(1024)(128)(4,1)}), s8[4194304]{0:T(1024)(128)(4,1)S(1)}, s32[]{:S(2)}) async-start(s8[16777216]{0:T(1024)(128)(4,1)} %bitcast.143), calls=%async_computation.4 | async-start | bytes 8388608
  332.9 15.3 %slice-start.2 = ((s8[16777216]{0:T(1024)(128)(4,1)}), s8[4194304]{0:T(1024)(128)(4,1)S(1)}, s32[]{:S(2)}) async-start(s8[16777216]{0:T(1024)(128)(4,1)} %bitcast.143), calls=%async_computation.5 | async-start | bytes 8388608
  332.9 16.7 %slice-start.3 = ((s8[16777216]{0:T(1024)(128)(4,1)}), s8[4194304]{0:T(1024)(128)(4,1)S(1)}, s32[]{:S(2)}) async-start(s8[16777216]{0:T(1024)(128)(4,1)} %bitcast.143), calls=%async_computation.6 | async-start | bytes 8388608
  349.6 11.0 %copy-start.10 = (f32[1024,4,32]{0,2,1:T(8,128)S(1)}, f32[1024,4,32]{0,2,1:T(8,128)}, u32[]{:S(2)}) copy-start(f32[1024,4,32]{0,2,1:T(8,128)} %copy-done.9) | copy-start | bytes 1572868
  349.6 11.0 %copy-start.12 = (f32[1024,4,32]{0,2,1:T(8,128)S(1)}, f32[1024,4,32]{0,2,1:T(8,128)}, u32[]{:S(2)}) copy-start(f32[1024,4,32]{0,2,1:T(8,128)} %copy-done.11) | copy-start | bytes 1572868
  349.6 11.0 %copy-start.34 = (f32[1024,4]{0,1:T(4,128)S(1)}, f32[1024,4]{0,1:T(4,128)}, u32[]{:S(2)}) copy-start(f32[1024,4]{0,1:T(4,128)} %copy-done.33) | copy-start | bytes 49156
  360.6 6.3 %copy-start.2 = (bf16[4,1024,1024]{1,2,0:T(8,128)(2,1)S(1)}, bf16[4,1024,1024]{1,2,0:T(8,128)(2,1)}, u32[]{:S(2)}) copy-start(bf16[4,1024,1024]{1,2,0:T(8,128)(2,1)} %multiply_convert_fusion) | copy-start | bytes 25165828
  360.6 6.3 %copy-start.6 = (f32[1024,4,32]{0,2,1:T(8,128)S(1)}, f32[1024,4,32]{0,2,1:T(8,128)}, u32[]{:S(2)}) copy-start(f32[1024,4,32]{0,2,1:T(8,128)} %copy-done.5) | copy-start | bytes 1572868
  360.7 6.3 %copy-start.8 = (f32[1024,4,32]{0,2,1:T(8,128)S(1)}, f32[1024,4,32]{0,2,1:T(8,128)}, u32[]{:S(2)}) copy-start(f32[1024,4,32]{0,2,1:T(8,128)} %copy-done.7) | copy-start | bytes 1572868
  360.7 6.3 %copy-start.36 = (f32[1024,4]{0,1:T(4,128)S(1)}, f32[1024,4]{0,1:T(4,128)}, u32[]{:S(2)}) copy-start(f32[1024,4]{0,1:T(4,128)} %copy-done.35) | copy-start | bytes 49156
  366.9 3.9 copy-start.49
  366.9 3.9 copy-start.47
  375.2 8.6 %copy-start.40 = (bf16[2,4,128,1024]{3,2,1,0:T(8,128)(2,1)S(1)}, bf16[2,4,128,1024]{3,2,1,0:T(8,128)(2,1)}, u32[]{:S(2)}) copy-start(bf16[2,4,128,1024]{3,2,1,0:T(8,128)(2,1)} %get-tuple-element.34) | copy-start | bytes 6291460
  393.2 20.2 %copy-start.56 = (f32[4352]{0:T(1024)S(1)}, f32[4352]{0:T(1024)}, u32[]{:S(2)}) copy-start(f32[4352]{0:T(1024)} %custom-call) | copy-start | bytes 52228
  393.2 20.2 %copy-start.66 = (f32[256]{0:T(256)S(1)}, f32[256]{0:T(256)}, u32[]{:S(2)}) copy-start(f32[256]{0:T(256)} %add.152) | copy-start | bytes 3076
  393.3 20.2 %copy-start.68 = (f32[1024]{0:T(1024)S(1)}, f32[1024]{0:T(1024)}, u32[]{:S(2)}) copy-start(f32[1024]{0:T(1024)} %get-tuple-element.53) | copy-start | bytes 12292
  393.3 20.2 %copy-start.67 = (f32[1024]{0:T(1024)S(1)}, f32[1024]{0:T(1024)}, u32[]{:S(2)}) copy-start(f32[1024]{0:T(1024)} %get-tuple-element.52) | copy-start | bytes 12292
  393.3 20.2 %copy-start.61 = (f32[1024]{0:T(1024)S(1)}, f32[1024]{0:T(1024)}, u32[]{:S(2)}) copy-start(f32[1024]{0:T(1024)} %get-tuple-element.58) | copy-start | bytes 12292
  393.3 20.3 %copy-start.57 = (f32[1024]{0:T(1024)S(1)}, f32[1024]{0:T(1024)}, u32[]{:S(2)}) copy-start(f32[1024]{0:T(1024)} %get-tuple-element.54) | copy-start | bytes 12292
  393.3 20.9 %copy-start.15 = (f32[2,128,1024]{2,1,0:T(8,128)S(1)}, f32[2,128,1024]{2,1,0:T(8,128)}, u32[]{:S(2)}) copy-start(f32[2,128,1024]{2,1,0:T(8,128)} %copy-done.14) | copy-start | bytes 3145732
  393.3 23.2 %copy-start.28 = (bf16[2,128,1024]{2,1,0:T(8,128)(2,1)S(1)}, bf16[2,128,1024]{2,1,0:T(8,128)(2,1)}, u32[]{:S(2)}) copy-start(bf16[2,128,1024]{2,1,0:T(8,128)(2,1)} %copy-done.27) | copy-start | bytes 1572868
  490.3 8.5 %copy-start.31 = (bf16[2,128,2048]{2,1,0:T(8,128)(2,1)S(1)}, bf16[2,128,2048]{2,1,0:T(8,128)(2,1)}, u32[]{:S(2)}) copy-start(bf16[2,128,2048]{2,1,0:T(8,128)(2,1)} %get-tuple-element.50) | copy-start | bytes 3145732
  (18 other events, 38.3 us)
Sparse Core Ops, SparseCore 0:
  51.9 91.9 all-gather.1
  238.9 111.9 reduce-scatter.1

commit v2 on v0

--- a/solution.py
+++ b/solution.py
@@ -5,10 +5,12 @@
 import jax.numpy as jnp
 from jax import lax
 from jax.experimental import pallas as pl
+from jax.experimental.layout import Layout, with_layout_constraint
 from jax.experimental.pallas import tpu as pltpu
 from jax.sharding import PartitionSpec as P
 
 HD = 64
+BLK = 256
 norm_eps = 1e-06
 rope_base = 10000.0
 BF = jnp.bfloat16
@@ -334,13 +336,11 @@
     n,
     g_ref,
     v_ref,
-    down_ref,
-    ug_ref,
+    early_ref,
     input_ref,
     out_ref,
     sums_ref,
-    full_down_ref,
-    full_ug_ref,
+    full_early_ref,
     traded_ref,
     arrived,
     reduced,
@@ -379,13 +379,11 @@
         near[d].start()
     shares = [
         remote(input_ref.at[other], traded_ref.at[ctx], share_send.at[0], share_receive.at[0], ctx=other),
-        remote(down_ref, full_down_ref.at[ctx], share_send.at[1], share_receive.at[1], ctx=other),
-        remote(ug_ref, full_ug_ref.at[ctx], share_send.at[2], share_receive.at[2], ctx=other),
+        remote(early_ref, full_early_ref.at[ctx], share_send.at[1], share_receive.at[1], ctx=other),
     ]
     own = [
         pltpu.make_async_copy(input_ref.at[ctx], traded_ref.at[ctx], local.at[0]),
-        pltpu.make_async_copy(down_ref, full_down_ref.at[ctx], local.at[1]),
-        pltpu.make_async_copy(ug_ref, full_ug_ref.at[ctx], local.at[2]),
+        pltpu.make_async_copy(early_ref, full_early_ref.at[ctx], local.at[1]),
     ]
     for copy in shares + own:
         copy.start()
@@ -451,21 +449,20 @@
     last.wait_send()
 
 
-def sum_grads(n, parts, vectors, down_share, ug_share, traded):
+def sum_grads(n, parts, vectors, early, traded):
     total_rows, width = parts.shape
     rows = total_rows // (2 * n)
     vector = pltpu.VMEM(vectors.shape, F32)
-    out, sums, down, ug, traded = pl.pallas_call(
+    out, sums, early, traded = pl.pallas_call(
         functools.partial(grads_kernel, n),
         out_shape=(
             jax.ShapeDtypeStruct((2, rows, width), BF),
             jax.ShapeDtypeStruct((4,) + vectors.shape, F32),
-            jax.ShapeDtypeStruct((2,) + down_share.shape, BF),
-            jax.ShapeDtypeStruct((2,) + ug_share.shape, BF),
+            jax.ShapeDtypeStruct((2,) + early.shape, BF),
             jax.ShapeDtypeStruct(traded.shape, BF),
         ),
-        in_specs=[IN_VMEM] * 5,
-        out_specs=(IN_VMEM,) * 5,
+        in_specs=[IN_VMEM] * 4,
+        out_specs=(IN_VMEM,) * 4,
         scratch_shapes=[
             pltpu.VMEM((n, rows, width), BF),
             pltpu.VMEM((n, rows, width), BF),
@@ -478,19 +475,18 @@
             pltpu.SemaphoreType.DMA((2 * n,)),
             pltpu.SemaphoreType.DMA((n + 3,)),
             pltpu.SemaphoreType.DMA((n + 3,)),
-            pltpu.SemaphoreType.DMA((3,)),
-            pltpu.SemaphoreType.DMA((3,)),
-            pltpu.SemaphoreType.DMA((3,)),
+            pltpu.SemaphoreType.DMA((2,)),
+            pltpu.SemaphoreType.DMA((2,)),
+            pltpu.SemaphoreType.DMA((2,)),
         ],
         compiler_params=pltpu.CompilerParams(collective_id=3, has_side_effects=True),
         cost_estimate=pl.CostEstimate(flops=0, bytes_accessed=120_000_000, transcendentals=0),
         name="sum_grads",
-    )(parts.reshape(n, 2, rows, width), vectors, down_share, ug_share, traded)
+    )(parts.reshape(n, 2, rows, width), vectors, early, traded)
     return (
         out.reshape(2 * rows, width),
         sums,
-        down.reshape(-1, down.shape[2]),
-        ug.reshape(-1, ug.shape[2]),
+        early.reshape(-1, early.shape[2]),
         traded,
     )
 
@@ -557,52 +553,117 @@
     return lax.all_to_all(values, "ctx", split_axis=0, concat_axis=0, tiled=True)
 
 
+def tiles_of(length):
+    return [pl.ds(i * BLK, BLK) for i in range(length // BLK)]
+
+
+def scores_of(keys, query, col_ref, row_ref, tiles, a, j):
+    scores = jnp.dot(keys[tiles[j], :], query, preferred_element_type=F32)
+    if j >= a:
+        scores = jnp.where(col_ref[tiles[j], :] <= row_ref[:, tiles[a]], scores, -1e30)
+    return scores
+
+
+def attend_kernel(q_ref, k_ref, v_ref, col_ref, row_ref, o_ref, lse_ref, keys):
+    tiles = tiles_of(q_ref.shape[2])
+
+    def one_head(h, carry):
+        keys[...] = k_ref[h].T
+        for a in range(len(tiles)):
+            query = q_ref[h, :, tiles[a]]
+            total = jnp.zeros((1, BLK), F32)
+            out = jnp.zeros((HD, BLK), F32)
+            for j in range(min(a + 2, len(tiles))):
+                soft = jnp.exp(scores_of(keys, query, col_ref, row_ref, tiles, a, j))
+                total += jnp.sum(soft, axis=0, keepdims=True)
+                out += jnp.dot(v_ref[h, :, tiles[j]], soft.astype(BF), preferred_element_type=F32)
+            o_ref[h, :, tiles[a]] = (out / total).astype(BF)
+            lse_ref[h, :, tiles[a]] = jnp.log(total)
+        return carry
+
+    lax.fori_loop(0, q_ref.shape[0], one_head, 0)
+
+
+def attend_both(query, key, value, ids):
+    heads, _, length = query.shape
+    return pl.pallas_call(
+        attend_kernel,
+        out_shape=(
+            jax.ShapeDtypeStruct(query.shape, BF),
+            jax.ShapeDtypeStruct((heads, 1, length), F32),
+        ),
+        in_specs=[IN_VMEM] * 5,
+        out_specs=(IN_VMEM,) * 2,
+        scratch_shapes=[pltpu.VMEM((length, HD), BF)],
+        cost_estimate=pl.CostEstimate(flops=10**9, bytes_accessed=3 * 10**7, transcendentals=0),
+        name="attend",
+    )(query, key, value, ids[:, None], ids[None, :])
+
+
+def attend_back_kernel(
+    q_ref, k_ref, v_ref, col_ref, row_ref, lse_ref, o_ref, g_ref, dq_ref, dk_ref, dv_ref, keys, values
+):
+    tiles = tiles_of(q_ref.shape[2])
+    last = (((1,), (1,)), ((), ()))
+
+    def one_head(h, carry):
+        keys[...] = k_ref[h].T
+        values[...] = v_ref[h].T
+        dk_ref[h] = jnp.zeros_like(dk_ref[h])
+        dv_ref[h] = jnp.zeros_like(dv_ref[h])
+        for a in range(len(tiles)):
+            query = q_ref[h, :, tiles[a]]
+            grad = g_ref[h, :, tiles[a]]
+            lse = lse_ref[h, :, tiles[a]]
+            delta = jnp.sum(
+                grad.astype(F32) * o_ref[h, :, tiles[a]].astype(F32), axis=0, keepdims=True
+            )
+            dq = jnp.zeros((HD, BLK), F32)
+            for j in range(min(a + 2, len(tiles))):
+                scores = scores_of(keys, query, col_ref, row_ref, tiles, a, j)
+                soft = jnp.exp(scores - lse)
+                dp = jnp.dot(values[tiles[j], :], grad, preferred_element_type=F32)
+                low = (soft * (dp - delta)).astype(BF)
+                dv_ref[h, :, tiles[j]] += lax.dot_general(
+                    grad, soft.astype(BF), last, preferred_element_type=F32
+                )
+                dk_ref[h, :, tiles[j]] += lax.dot_general(
+                    query, low, last, preferred_element_type=F32
+                )
+                dq += jnp.dot(k_ref[h, :, tiles[j]], low, preferred_element_type=F32)
+            dq_ref[h, :, tiles[a]] = dq * (1 / math.sqrt(HD))
+        return carry
+
+    lax.fori_loop(0, q_ref.shape[0], one_head, 0)
+
+
+def attend_back(query, key, value, ids, logsum, out, grad):
+    heads, _, length = query.shape
+    shape = jax.ShapeDtypeStruct(query.shape, F32)
+    return pl.pallas_call(
+        attend_back_kernel,
+        out_shape=(shape,) * 3,
+        in_specs=[IN_VMEM] * 8,
+        out_specs=(IN_VMEM,) * 3,
+        scratch_shapes=[pltpu.VMEM((length, HD), BF)] * 2,
+        cost_estimate=pl.CostEstimate(flops=3 * 10**9, bytes_accessed=6 * 10**7, transcendentals=0),
+        name="attend_back",
+    )(query, key, value, ids[:, None], ids[None, :], logsum, out, grad)
+
+
+def tokens_minor(values):
+    return values.T.reshape(-1, HD, values.shape[0])
+
+
+def tokens_major(values):
+    return values.reshape(-1, values.shape[2]).T
+
+
 def swap_halves(share, ctx):
     got = lax.ppermute(share, "ctx", [(0, 1), (1, 0)])
     first = jnp.where(ctx == 0, share, got)
     second = jnp.where(ctx == 0, got, share)
     return jnp.concatenate([first, second], axis=0)
-
-
-def attend_both(query_low, key_low, value_low, ids):
-    length, width = query_low.shape
-    heads = width // HD
-    q = query_low.reshape(length, heads, HD)
-    k = key_low.reshape(length, heads, HD)
-    v = value_low.reshape(length, heads, HD)
-    scores = jnp.einsum("qhd,khd->hqk", q, k, preferred_element_type=F32) / math.sqrt(HD)
-    allowed = ids[None, :] <= ids[:, None]
-    scores = jnp.where(allowed[None], scores, -1e30)
-    row_max = jnp.max(scores, axis=-1, keepdims=True)
-    exponent = jnp.exp(scores - row_max)
-    row_total = jnp.sum(exponent, axis=-1, keepdims=True)
-    weights_low = (exponent / row_total).astype(BF)
-    out = jnp.einsum("hqk,khd->qhd", weights_low, v, preferred_element_type=F32)
-    return out.reshape(length, width).astype(BF), (row_max + jnp.log(row_total))[..., 0]
-
-
-def attend_back(query_low, key_low, value_low, ids, logsum, grad):
-    length, width = query_low.shape
-    heads = width // HD
-    q = query_low.reshape(length, heads, HD)
-    k = key_low.reshape(length, heads, HD)
-    v = value_low.reshape(length, heads, HD)
-    g = grad.reshape(length, heads, HD)
-    scores = jnp.einsum("qhd,khd->hqk", q, k, preferred_element_type=F32) / math.sqrt(HD)
-    allowed = ids[None, :] <= ids[:, None]
-    scores = jnp.where(allowed[None], scores, -1e30)
-    soft = jnp.exp(scores - logsum[..., None])
-    grad_v = jnp.einsum("hqk,qhd->khd", soft.astype(BF), g, preferred_element_type=F32)
-    grad_w = jnp.einsum("qhd,khd->hqk", g, v, preferred_element_type=F32)
-    grad_s = soft * (grad_w - jnp.sum(grad_w * soft, axis=-1, keepdims=True))
-    low = grad_s.astype(BF)
-    grad_q = jnp.einsum("hqk,khd->qhd", low, k, preferred_element_type=F32) / math.sqrt(HD)
-    grad_k = jnp.einsum("hqk,qhd->khd", low, q, preferred_element_type=F32) / math.sqrt(HD)
-    return (
-        grad_q.reshape(length, width),
-        grad_k.reshape(length, width),
-        grad_v.reshape(length, width),
-    )
 
 
 def per_device(sizes):
@@ -639,7 +700,7 @@
             return lax.dynamic_slice_in_dim(shard, ctx * half, half, 0)
 
         ug_half = own_half(jnp.concatenate([up_weight, gate_weight], axis=1))
-        down_half = own_half(down_weight.T)
+        down_half = with_layout_constraint(own_half(down_weight.T), Layout((0, 1)))
         if small:
             gathered, full_qkv, full_output = opening(
                 n, residual, query_weight, key_weight, value_weight, output_weight
@@ -669,10 +730,11 @@
 
         query_ready, query_back = jax.vjp(prepare_local, raw_query, sharpness)
         key_ready, key_back = jax.vjp(prepare_local, raw_key, sharpness)
-        query_low = query_ready.astype(BF)
-        key_low = key_ready.astype(BF)
-        value_low = raw_value.astype(BF)
+        query_low = tokens_minor(query_ready.astype(BF) * BF(1 / math.sqrt(HD)))
+        key_low = tokens_minor(key_ready.astype(BF))
+        value_low = tokens_minor(raw_value.astype(BF))
         attended, logsum = attend_both(query_low, key_low, value_low, ids)
+        flat_attended = attended.reshape(heads_width, -1)
 
         def reduce_rows(partial):
             return tensor_scatter(partial.astype(BF).reshape(shape4))
@@ -680,7 +742,7 @@
         def gather_rows(values):
             return tensor_gather(values.astype(BF)).reshape(-1, width)
 
-        attend_sum = reduce_rows(product(attended, full_output))
+        attend_sum = reduce_rows(transposed_left(flat_attended, full_output))
         residual_float = mine.astype(F32)
         first, attend_back_mix = jax.vjp(branch_mix, attend_sum, residual_float, attend_rate)
         first_all = gather_rows(first)
@@ -704,11 +766,20 @@
         grad_ug_part = transposed_left(first_all, ug_grad)
         grad_attend_sum, grad_residual, grad_attend_part = attend_back_mix(grad_first)
         attend_grad_all = gather_rows(grad_attend_sum)
-        grad_output_part = transposed_left(attend_grad_all, attended)
-        grad_attended = transposed_right(attend_grad_all, full_output).astype(BF)
-        grad_query_ready, grad_key_ready, grad_value_ready = attend_back(
-            query_low, key_low, value_low, ids, logsum, grad_attended
-        )
+        grad_output_part = product(flat_attended, attend_grad_all).T
+        grad_attended = transposed_right(full_output, attend_grad_all).astype(BF)
+        grad_query_ready, grad_key_ready, grad_value_ready = [
+            tokens_major(part)
+            for part in attend_back(
+                query_low,
+                key_low,
+                value_low,
+                ids,
+                logsum,
+                attended,
+                grad_attended.reshape(attended.shape),
+            )
+        ]
         grad_raw_query, sharp_query = query_back(grad_query_ready)
         grad_raw_key, sharp_key = key_back(grad_key_ready)
         qkv_grad = jnp.concatenate(
@@ -733,22 +804,20 @@
         lengths = [vector.shape[0] for vector in vectors]
         packed = jnp.concatenate(vectors)
         packed = jnp.pad(packed, (0, -packed.shape[0] % 1024)).reshape(-1, 128)
-        down_share = scatter_rows(grad_down_part)
-        ug_share = scatter_rows(grad_ug_part)
+        early = scatter_rows(
+            jnp.concatenate([grad_down_part.astype(BF), grad_ug_part.astype(BF)], axis=1)
+        )
         late = jnp.concatenate([grad_qkv_part.astype(BF), grad_output_part.astype(BF)], axis=1)
         if small:
-            late, sums, grad_down, grad_ug, grad_input = sum_grads(
-                n, late, packed, down_share, ug_share, grad_input
-            )
+            late, sums, early, grad_input = sum_grads(n, late, packed, early, grad_input)
         else:
             late = swap_halves(scatter_rows(late), ctx)
             sums = lax.all_gather(lax.psum(packed, ("fsdp", "ctx")), "tp", axis=0)
-            grad_down = swap_halves(down_share, ctx)
-            grad_ug = swap_halves(ug_share, ctx)
+            early = swap_halves(early, ctx)
             grad_input = trade(grad_input, sizes)
         late = late.astype(F32)
-        grad_down = grad_down.astype(F32).T
-        grad_ug = grad_ug.astype(F32)
+        grad_down = early[:, :hidden_here].astype(F32).T
+        grad_ug = early[:, hidden_here:].astype(F32)
         grad_input = grad_input.astype(F32)
         grad_up, grad_gate = grad_ug[:, :hidden_here], grad_ug[:, hidden_here:]
         grad_query, grad_key, grad_value = jnp.split(late[:, : 3 * heads_width], 3, axis=1)

time: 474 us -> 448 us (0.945)
  matrix products: 110 us -> 57.6 us
  Pallas kernels: 225 us -> 250 us
  waiting for transfers between devices: 24.8 us -> 42.9 us
  other arithmetic: 59.6 us -> 44 us
    dot_general x6 -> x0, matrix products: 49.6 us -> none  [the longest x1 14.9 us: attend_back(): grad_w = jnp.einsum('qhd,khd->hqk', g, v, preferred_element_type=F32)]
    pallas_call x0 -> x2, Pallas kernels: none -> 27.1 us  [the longest x1 17.5 us: attend_back(): pl.pallas_call(attend_back_kernel, out_shape=(shape,) * 3, in_specs=[IN_V...]
    all_gather x1, waiting for transfers between devices: 24.4 us -> 37.8 us  [run(): full_down = lax.all_gather(down_half, ('fsdp', 'ctx'), axis=0, tiled=True)]
    convert_element_type x2 -> x3, other arithmetic: 11.3 us -> 3.93 us  [the longest x1 1.49 us: run(): grad_ug = early[:, hidden_here:].astype(F32)]
    reduce_sum x1 -> x2, other arithmetic: 8.06 us -> 1.95 us  [prepare_heads(): unit_rows(rotate_pairs(shaped, angles))]
    unnamed x169 -> x174, local copies, waits for them, and re-layouts: 17.2 us -> 16.5 us
  transfers between devices with their start and end apart: 7 -> 6, of which waited for: 2 -> 3; matrix products, arithmetic and copies ran while one was open for 33% -> 17% of each run, Pallas kernels for 19% -> 27%
where the time goes in v2:
time: 448 us; the launch traced here: 443 us
  Pallas kernels  250 us (56%)
  matrix products  57.6 us (13%)
  other arithmetic  44 us (10%)
  waiting for transfers between devices  42.9 us (10%)
  local copies, waits for them, and re-layouts  30.7 us (7%)
  between operations  15.2 us (3%)
    pallas_call x4, Pallas kernels, tensor_scatter(): pl.pallas_call(functools.partial(scatter_kernel, chunks), out_shape=jax.S...  74.2 us
    pallas_call x1, Pallas kernels, sum_grads(): pl.pallas_call(functools.partial(grads_kernel, n), out_shape=(jax.ShapeDt...  56.8 us
    pallas_call x3, Pallas kernels, tensor_gather(): pl.pallas_call(functools.partial(gather_kernel, chunks), out_shape=jax.Sh...  52.2 us
    pallas_call x1, Pallas kernels, opening(): pl.pallas_call(functools.partial(opening_kernel, n), out_shape=(jax.Shape...  39.3 us
    all_gather x1, waiting for transfers between devices, run(): full_down = lax.all_gather(down_half, ('fsdp', 'ctx'), axis=0, tiled=True)  37.8 us
    dot_general x4, matrix products, transposed_right(): lax.dot_general(left, right, (((1,), (1,)), ((), ())), preferred_element_...  21.7 us
    dot_general x4, matrix products, product(): return jnp.dot(left, right, preferred_element_type=F32)  21 us
    pallas_call x1, Pallas kernels, attend_back(): pl.pallas_call(attend_back_kernel, out_shape=(shape,) * 3, in_specs=[IN_V...  17.5 us
  transfers between devices with their start and end apart: 6, of which 3 were waited for; matrix products, arithmetic and copies ran while one was open for 17% of the time, Pallas kernels for 27%

profile of v2, /device:TPU:0, one launch (start us, length us, event | category | flops | bytes accessed | tf_op | source)
XLA Modules:
  0.0 442.9 jit_solution(6264349583948423309)
XLA Ops:
  7.2 1.0 copy-done
  8.3 0.9 copy.45
  9.1 1.9 fusion.13
  11.0 39.3 %opening.1 = (bf16[2,4,128,1024]{3,2,1,0:T(8,128)(2,1)}, bf16[4,256,768]{2,1,0:T(8,128)(2,1)}, bf16[256,1024]{1,0:T(8,128)(2,1)}) custom-call(bf16[2,128,1024]{2,1,0:T(8,128)(2,1)} %x_ref.1, bf16[256,256]{1,0:T(8,128)(2,1)} %q_ref.1, bf16[256,256]{1,0:T(8,128)(2,1)} %k_ref.1, bf16[256,256]{1,0:T(8,128)(2,1)} %v_ref.1, bf16[256,256]{1,0:T(8,128)(2,1)} %o_ref.1), custom_call_target="tpu_custom_call" | custom-call | bytes 60000000 | tf_op jit(solution)/shard_map/opening/pallas_call | solution.py:314
  51.7 1.5 collective-permute-start.2
  53.9 3.9 fusion.33
  57.9 1.6 copy-done.21
  59.8 2.1 split.60
  61.9 1.0 copy.38.col_ref
  65.3 1.1 fusion.10
  66.4 0.9 fusion.12
  67.4 9.6 %attend.1 = (bf16[4,64,1024]{2,1,0:T(8,128)(2,1)}, f32[4,1,1024]{2,1,0:T(1,128)}) custom-call(bf16[4,64,1024]{2,1,0:T(8,128)(2,1)} %bitcast.183, bf16[4,64,1024]{2,1,0:T(8,128)(2,1)} %bitcast.181, bf16[4,64,1024]{2,1,0:T(8,128)(2,1)} %bitcast.175, s32[1024,1]{1,0:T(8,128)} %copy.38.col_ref, s32[1,1024]{1,0:T(1,128)} %constant_dynamic-slice_fusion.row_ref), custom_call_target="tpu_custom_call" | custom-call | flops 1000000000 | bytes 30000000 | tf_op jit(solution)/shard_map/attend/pallas_call | solution.py:589
  77.0 3.1 convolution_convert_fusion.3
  80.1 18.6 %tensor_scatter.4 = f32[2,128,1024]{2,1,0:T(8,128)} custom-call(bf16[2,4,128,1024]{3,2,1,0:T(8,128)(2,1)} %bitcast.153), custom_call_target="tpu_custom_call" | custom-call | bytes 40000000 | tf_op jit(solution)/shard_map/tensor_scatter/pallas_call | solution.py:188
  98.7 1.4 multiply_reduce_fusion.12
  100.6 1.8 multiply_reduce_fusion.11
  102.5 0.9 multiply_convert_fusion.4.x_ref
  103.4 17.2 %tensor_gather.3 = bf16[2,4,128,1024]{3,2,1,0:T(8,128)(2,1)} custom-call(bf16[2,128,1024]{2,1,0:T(8,128)(2,1)} %multiply_convert_fusion.4.x_ref), custom_call_target="tpu_custom_call" | custom-call | bytes 40000000 | tf_op jit(solution)/shard_map/tensor_gather/pallas_call | solution.py:111
  120.6 1.7 fusion.14
  122.3 1.0 all-gather.3.cloned.1.call-done
  123.2 6.9 %fusion.34 = f32[1024,2048]{1,0:T(8,128)S(1)} fusion(bf16[1024,1024]{1,0:T(8,128)(2,1)} %bitcast.159, bf16[1024,2048]{1,0:T(8,128)(2,1)} %all-gather.3.cloned.1.call-done), kind=kOutput, calls=%fused_computation.153 | convolution fusion | flops 4294967296 | bytes 14680064 | tf_op jit(solution)/shard_map/dot_general | solution.py:523
  130.2 3.3 copy-done.19
  133.5 2.3 multiply_convert_fusion.2
  135.8 37.8 %all-gather.5.cloned.1.call-done = bf16[1024,1024]{1,0:T(8,128)(2,1)} async-done(((bf16[128,1024]{1,0:T(8,128)(2,1)}), bf16[1024,1024]{1,0:T(8,128)(2,1)}) %all-gather.5.cloned.1.call-update) | async-done | bytes 2097168 | tf_op jit(solution)/shard_map/all_gather | solution.py:718
  173.6 5.9 %convolution_convert_fusion.2 = bf16[1024,1024]{1,0:T(8,128)(2,1)} fusion(bf16[1024,1024]{1,0:T(8,128)(2,1)} %multiply_convert_fusion.2, bf16[1024,1024]{1,0:T(8,128)(2,1)} %all-gather.5.cloned.1.call-done), kind=kOutput, calls=%fused_computation.19 | convolution fusion | flops 2148532224 | bytes 6291456 | tf_op jit(solution)/shard_map/dot_general | solution.py:531
  179.5 18.5 %tensor_scatter.5 = f32[2,128,1024]{2,1,0:T(8,128)} custom-call(bf16[2,4,128,1024]{3,2,1,0:T(8,128)(2,1)} %bitcast.165), custom_call_target="tpu_custom_call" | custom-call | bytes 40000000 | tf_op jit(solution)/shard_map/tensor_scatter/pallas_call | solution.py:188
  198.1 1.5 multiply_reduce_fusion.10
  199.6 1.8 fusion.5
  202.1 1.4 fusion.6.x_ref
  203.5 17.6 %tensor_gather.4 = bf16[2,4,128,1024]{3,2,1,0:T(8,128)(2,1)} custom-call(bf16[2,128,1024]{2,1,0:T(8,128)(2,1)} %fusion.6.x_ref), custom_call_target="tpu_custom_call" | custom-call | bytes 40000000 | tf_op jit(solution)/shard_map/tensor_gather/pallas_call | solution.py:111
  221.2 4.8 %convolution_convert_fusion.1 = bf16[1024,1024]{1,0:T(8,128)(2,1)S(1)} fusion(bf16[1024,1024]{1,0:T(8,128)(2,1)} %bitcast.161, bf16[1024,1024]{1,0:T(8,128)(2,1)} %multiply_convert_fusion.2), kind=kOutput, calls=%fused_computation.18 | convolution fusion | flops 2148532224 | bytes 6291456 | tf_op jit(solution)/shard_map/dot_general | solution.py:527
  226.0 7.7 %multiply_reduce_fusion = (f32[1024]{0:T(1024)}, f32[1024]{0:T(1024)}, f32[1024,1024]{1,0:T(8,128)S(1)}, bf16[1024,1024]{1,0:T(8,128)(2,1)S(1)}) fusion(f32[1024,2048]{1,0:T(8,128)} %copy-done.19, f32[1024]{0:T(1024)S(1)} %copy-done.63, f32[1024]{0:T(1024)S(1)} %copy-done.74, bf16[1024,1024]{1,0:T(8,128)(2,1)S(1)} %bitcast.162, ...), kind=kOutput, calls=%fused_computation.5 | convolution fusion | flops 2168453120 | bytes 18890752 | tf_op jit(solution)/shard_map/dot_general | solution.py:523
  235.0 1.8 copy-done.22
  236.8 5.2 %convolution_convert_fusion = bf16[1024,2048]{1,0:T(8,128)(2,1)S(1)} fusion(bf16[1024,1024]{1,0:T(8,128)(2,1)S(1)} %bitcast.160, bf16[1024,1024]{1,0:T(8,128)(2,1)S(1)} %multiply_convert_fusion, bf16[1024,1024]{1,0:T(8,128)(2,1)S(1)} %get-tuple-element.60), kind=kOutput, calls=%fused_computation.14 | convolution fusion | flops 4305453056 | bytes 10485760 | tf_op jit(solution)/shard_map/dot_general | solution.py:527
  242.0 3.3 pad_maximum_fusion
  245.3 1.3 mul.570
  246.6 9.3 %fusion.4 = bf16[1024,1024]{1,0:T(8,128)(2,1)} fusion(bf16[1024,2048]{1,0:T(8,128)(2,1)} %all-gather.3.cloned.1.call-done, bf16[1024,1024]{1,0:T(8,128)(2,1)} %copy-done.24, bf16[1024,1024]{1,0:T(8,128)(2,1)} %copy-done.80), kind=kOutput, calls=%fused_computation.17 | convolution fusion | flops 4304404480 | bytes 10485760 | tf_op jit(solution)/shard_map/dot_general | solution.py:531
  256.0 18.5 %tensor_scatter.6 = f32[2,128,1024]{2,1,0:T(8,128)} custom-call(bf16[2,4,128,1024]{3,2,1,0:T(8,128)(2,1)} %bitcast.163), custom_call_target="tpu_custom_call" | custom-call | bytes 40000000 | tf_op jit(solution)/shard_map/tensor_scatter/pallas_call | solution.py:188
  274.6 2.8 multiply_reduce_fusion.2
  277.6 3.6 multiply_reduce_fusion.3
  281.2 0.9 copy-done.11
  282.2 1.0 fusion.7.x_ref
  283.2 17.4 %tensor_gather.5 = bf16[2,4,128,1024]{3,2,1,0:T(8,128)(2,1)} custom-call(bf16[2,128,1024]{2,1,0:T(8,128)(2,1)} %fusion.7.x_ref), custom_call_target="tpu_custom_call" | custom-call | bytes 40000000 | tf_op jit(solution)/shard_map/tensor_gather/pallas_call | solution.py:111
  300.7 3.3 convolution_convert_fusion.7
  303.9 17.5 %attend_back.1 = (f32[4,64,1024]{2,1,0:T(8,128)}, f32[4,64,1024]{2,1,0:T(8,128)}, f32[4,64,1024]{2,1,0:T(8,128)}) custom-call(bf16[4,64,1024]{2,1,0:T(8,128)(2,1)} %bitcast.184, bf16[4,64,1024]{2,1,0:T(8,128)(2,1)} %bitcast.182, bf16[4,64,1024]{2,1,0:T(8,128)(2,1)} %bitcast.176, s32[1024,1]{1,0:T(8,128)} %copy.38.col_ref, ...), custom_call_target="tpu_custom_call" | custom-call | flops 3000000000 | bytes 60000000 | tf_op jit(solution)/shard_map/attend_back/pallas_call | solution.py:643
  321.4 1.4 convert_element_type.143
  322.9 1.7 multiply_reduce_fusion.5
  326.1 1.2 copy-done.79
  327.4 3.2 convolution_convert_fusion.4
  330.5 18.7 %tensor_scatter.7 = f32[2,128,1024]{2,1,0:T(8,128)} custom-call(bf16[2,4,128,1024]{3,2,1,0:T(8,128)(2,1)} %bitcast.164), custom_call_target="tpu_custom_call" | custom-call | bytes 40000000 | tf_op jit(solution)/shard_map/tensor_scatter/pallas_call | solution.py:188
  349.3 2.4 convolution_convert_fusion.6
  351.7 1.8 convolution_convert_fusion.5
  353.6 1.5 pad_maximum_fusion.4
  355.1 4.1 copy.40
  359.8 1.8 fusion.8
  362.5 1.0 add_convert_fusion.input_ref
  363.5 4.1 collective-permute-done.1
  368.6 56.8 %sum_grads.1 = (bf16[2,128,1024]{2,1,0:T(8,128)(2,1)}, f32[4,40,128]{2,1,0:T(8,128)}, bf16[2,128,3072]{2,1,0:T(8,128)(2,1)}, bf16[2,128,1024]{2,1,0:T(8,128)(2,1)}) custom-call(bf16[4,2,128,1024]{3,2,1,0:T(8,128)(2,1)} %bitcast.154, f32[40,128]{1,0:T(8,128)} %pad_bitcast_fusion.v_ref, bf16[128,3072]{1,0:T(8,128)(2,1)} %reduce-scatter.2.cloned.1.call-done.early_ref, ...), custom_call_target="tpu_custom_call" | custom-call | bytes 120000000 | tf_op jit(solution)/shard_map/sum_grads/pallas_call | solution.py:456
  425.4 1.5 slice_convert_fusion
  426.9 1.1 slice.80
  428.6 1.4 fusion.31
  430.2 0.9 fusion.32
  432.2 1.0 convert_bitcast_fusion
  433.2 1.1 convert_element_type.152
  (219 shorter events, 14.9 us)
Async XLA Ops:
  7.2 116.0 %all-gather.3.cloned.1.call-start = ((), (), s32[]{:S(2)}) async-start(), calls=%async_computation.1 | async-start | bytes 4718592 | tf_op jit(solution)/shard_map/all_gather | solution.py:717
  8.2 42.2 %copy-start.75 = (s32[2,512]{1,0:T(2,128)S(1)}, s32[2,512]{1,0:T(2,128)}, u32[]{:S(2)}) copy-start(s32[2,512]{1,0:T(2,128)} %param.30) | copy-start | bytes 12292
  8.2 42.8 %copy-start.28 = (bf16[2,128,1024]{2,1,0:T(8,128)(2,1)S(1)}, bf16[2,128,1024]{2,1,0:T(8,128)(2,1)}, u32[]{:S(2)}) copy-start(bf16[2,128,1024]{2,1,0:T(8,128)(2,1)} %param.31) | copy-start | bytes 1572868
  9.1 44.2 %copy-start.72 = (s32[2,1024]{1,0:T(2,128)S(1)}, s32[2,1024]{1,0:T(2,128)}, u32[]{:S(2)}) copy-start(s32[2,1024]{1,0:T(2,128)} %param.29) | copy-start | bytes 24580
  50.3 123.3 %all-gather.5.cloned.1.call-start = ((), (), s32[]{:S(2)}) async-start(), calls=%async_computation.2 | async-start | bytes 2359296 | tf_op jit(solution)/shard_map/all_gather | solution.py:718
  50.4 12.5 %collective-permute-start = (s32[512]{0:T(512)S(1)}, s32[512]{0:T(512)S(1)}, u32[]{:S(2)}, u32[]{:S(2)}) collective-permute-start(s32[512]{0:T(512)S(1)} %bitcast.196), channel_id=1, source_target_pairs={{0,4},{4,0},{1,5},{5,1},{2,6},{6,2},{3,7},{7,3},{8,12},{12,8},{9,1... | collective-permute-start | bytes 6152 | tf_op jit(solution)/shard_map/ppermute | solution.py:549
  51.7 68.8 %collective-permute-start.2 = (bf16[128,1024]{1,0:T(8,128)(2,1)}, bf16[128,1024]{1,0:T(8,128)(2,1)}, u32[]{:S(2)}, u32[]{:S(2)}) collective-permute-start(bf16[128,1024]{1,0:T(8,128)(2,1)} %dynamic-slice_bitcast_fusion), channel_id=1, source_target_pairs={{0,4},{4,0},{1,5},{5,1},{2,6},{6,2},{3,7},{7,3},{8,12},{12,8},{9,1... | collective-permute-start | bytes 786440 | tf_op jit(solution)/shard_map/ppermute | solution.py:549
  53.3 315.3 %reduce-scatter.2.cloned.1.call-start = ((), (), s32[]{:S(2)}) async-start(), calls=%async_computation.3 | async-start | bytes 7077888 | tf_op jit(solution)/shard_map/reduce_scatter | solution.py:793
  64.6 2.7 copy-start.13
  65.2 2.2 copy-start.38
  67.4 9.6 %copy-start.35 = (bf16[256,1024]{1,0:T(8,128)(2,1)S(1)}, bf16[256,1024]{1,0:T(8,128)(2,1)}, u32[]{:S(2)}) copy-start(bf16[256,1024]{1,0:T(8,128)(2,1)} %get-tuple-element.33) | copy-start | bytes 1572868
  80.1 20.5 %copy-start.47 = (f32[1024]{0:T(1024)S(1)}, f32[1024]{0:T(1024)}, u32[]{:S(2)}) copy-start(f32[1024]{0:T(1024)} %param.22) | copy-start | bytes 12292
  100.6 2.8 copy-start.64
  102.4 18.1 %copy-start.67 = (f32[2,128]{1,0:T(2,128)}, f32[2,128]{1,0:T(2,128)S(1)}, u32[]{:S(2)}) copy-start(f32[2,128]{1,0:T(2,128)S(1)} %get-tuple-element.58) | copy-start | bytes 3076
  102.4 18.1 %copy-start.50 = (f32[2,128]{1,0:T(2,128)}, f32[2,128]{1,0:T(2,128)S(1)}, u32[]{:S(2)}) copy-start(f32[2,128]{1,0:T(2,128)S(1)} %fusion.22) | copy-start | bytes 3076
  102.5 18.1 %copy-start.29 = (bf16[2,128,1024]{2,1,0:T(8,128)(2,1)S(1)}, bf16[2,128,1024]{2,1,0:T(8,128)(2,1)}, u32[]{:S(2)}) copy-start(bf16[2,128,1024]{2,1,0:T(8,128)(2,1)} %param.31) | copy-start | bytes 1572868
  123.2 10.3 %copy-start.62 = (f32[1024]{0:T(1024)S(1)}, f32[1024]{0:T(1024)}, u32[]{:S(2)}) copy-start(f32[1024]{0:T(1024)} %param.27) | copy-start | bytes 12292
  123.2 10.3 %copy-start.73 = (f32[1024]{0:T(1024)S(1)}, f32[1024]{0:T(1024)}, u32[]{:S(2)}) copy-start(f32[1024]{0:T(1024)} %param.26) | copy-start | bytes 12292
  130.2 3.3 copy-start.19
  198.0 3.4 copy-start.2
  198.1 3.4 copy-start.8
  198.1 3.3 copy-start.44
  198.1 3.3 copy-start.51
  199.6 2.5 copy-start.53
  221.2 4.8 %copy-start.23 = (bf16[2,4,128,1024]{3,2,1,0:T(8,128)(2,1)S(1)}, bf16[2,4,128,1024]{3,2,1,0:T(8,128)(2,1)}, u32[]{:S(2)}) copy-start(bf16[2,4,128,1024]{3,2,1,0:T(8,128)(2,1)} %tensor_gather.4) | copy-start | bytes 6291460
  221.2 4.8 %copy-start.63 = (f32[1024]{0:T(1024)S(1)}, f32[1024]{0:T(1024)}, u32[]{:S(2)}) copy-start(f32[1024]{0:T(1024)} %param.27) | copy-start | bytes 12292
  221.2 4.8 %copy-start.74 = (f32[1024]{0:T(1024)S(1)}, f32[1024]{0:T(1024)}, u32[]{:S(2)}) copy-start(f32[1024]{0:T(1024)} %param.26) | copy-start | bytes 12292
  221.2 4.8 %copy-start.78 = (bf16[1024,1024]{1,0:T(8,128)(2,1)S(1)}, bf16[1024,1024]{1,0:T(8,128)(2,1)}, u32[]{:S(2)}) copy-start(bf16[1024,1024]{1,0:T(8,128)(2,1)} %all-gather.5.cloned.1.call-done) | copy-start | bytes 6291460
  233.7 3.1 copy-start.22
  234.3 7.7 %copy-start.24 = (bf16[1024,1024]{1,0:T(8,128)(2,1)}, bf16[1024,1024]{1,0:T(8,128)(2,1)S(1)}, u32[]{:S(2)}) copy-start(bf16[1024,1024]{1,0:T(8,128)(2,1)S(1)} %multiply_convert_fusion) | copy-start | bytes 6291460
  274.5 3.0 copy-start.68
  274.5 3.0 copy-start.3
  274.5 3.0 copy-start.9
  274.5 3.0 copy-start.10
  274.5 3.0 copy-start.45
  274.5 3.0 copy-start.48
  274.6 3.0 copy-start.52
  274.6 3.0 copy-start.54
  274.6 3.0 copy-start.56
  274.6 2.9 copy-start.58
  274.6 2.9 copy-start.65
  277.6 3.7 copy-start.70
  282.2 18.5 %copy-start.36 = (bf16[256,1024]{1,0:T(8,128)(2,1)S(1)}, bf16[256,1024]{1,0:T(8,128)(2,1)}, u32[]{:S(2)}) copy-start(bf16[256,1024]{1,0:T(8,128)(2,1)} %get-tuple-element.33) | copy-start | bytes 1572868
  303.9 18.9 %copy-start.5 = (f32[1024,4,32]{0,2,1:T(8,128)S(1)}, f32[1024,4,32]{0,2,1:T(8,128)}, u32[]{:S(2)}) copy-start(f32[1024,4,32]{0,2,1:T(8,128)} %copy-done.4) | copy-start | bytes 1572868
  303.9 18.9 %copy-start.7 = (f32[1024,4,32]{0,2,1:T(8,128)S(1)}, f32[1024,4,32]{0,2,1:T(8,128)}, u32[]{:S(2)}) copy-start(f32[1024,4,32]{0,2,1:T(8,128)} %copy-done.6) | copy-start | bytes 1572868
  303.9 18.9 %copy-start.60 = (f32[4,64]{1,0:T(4,128)S(1)}, f32[4,64]{1,0:T(4,128)}, u32[]{:S(2)}) copy-start(f32[4,64]{1,0:T(4,128)} %mul.570) | copy-start | bytes 3076
  322.8 3.4 copy-start.30
  330.5 18.7 %copy-start.37 = (bf16[4,64,1024]{2,1,0:T(8,128)(2,1)S(1)}, bf16[4,64,1024]{2,1,0:T(8,128)(2,1)}, u32[]{:S(2)}) copy-start(bf16[4,64,1024]{2,1,0:T(8,128)(2,1)} %get-tuple-element.32.o_ref) | copy-start | bytes 1572868
  349.2 2.5 copy-start.31
  349.3 2.5 copy-start.34
  355.1 4.1 copy-start.25
  355.1 4.8 %copy-start.14 = (f32[1024,4,64]{0,2,1:T(8,128)S(1)}, f32[1024,4,64]{0,2,1:T(8,128)}, u32[]{:S(2)}) copy-start(f32[1024,4,64]{0,2,1:T(8,128)} %copy-done.13) | copy-start | bytes 3145732
  359.2 2.4 copy-start.16
  359.2 2.6 copy-start.59
  359.2 2.6 copy-start.77
  359.2 2.6 copy-start.76
  359.3 2.6 copy-start.66
  359.3 2.6 copy-start.61
  359.3 3.2 copy-start.12
  359.3 3.2 copy-start.20
  359.3 3.2 copy-start.49
  359.3 8.4 %collective-permute-start.1 = (bf16[128,1024]{1,0:T(8,128)(2,1)S(1)}, bf16[128,1024]{1,0:T(8,128)(2,1)S(1)}, u32[]{:S(2)}, u32[]{:S(2)}) collective-permute-start(bf16[128,1024]{1,0:T(8,128)(2,1)S(1)} %dynamic-slice_bitcast_fusion.1), channel_id=1, source_target_pairs={{0,4},{4,0},{1,5},{5,1},{2,6},{6,2},{3,7},{7,3},{8,12},{12,8},{9,1... | collective-permute-start | bytes 786440 | tf_op jit(solution)/shard_map/ppermute | solution.py:549
  425.4 2.6 copy-start.46
  431.1 5.0 %copy-start.1 = (bf16[1024,256]{1,0:T(8,128)(2,1)S(1)}, bf16[1024,256]{1,0:T(8,128)(2,1)}, u32[]{:S(2)}) copy-start(bf16[1024,256]{1,0:T(8,128)(2,1)} %param.25) | copy-start | bytes 1572868
  (23 other events, 28.4 us)
Sparse Core Ops, SparseCore 0:
  50.5 72.7 all-gather.2
  125.9 47.6 all-gather.4
  245.4 115.8 reduce-scatter.1
